TPU v7x, 32 devices: a whole 2x2x4 slice. The times are simulated.
32 devices in a mesh: groups: 2 (over x), seq: 16 (over z, y, core).
Axes of the slice: x: 2, y: 2, z: 4, core: 2. Of those that a mesh axis runs over, the one named last changes fastest.
Arguments:
- layer_in: bfloat16 [8192, 2560], P(('groups', 'seq')), parts along dimension 0, may hold values from -6 to 6
- ssm_in: bfloat16 [8192, 2560], P(('groups', 'seq')), parts along dimension 0, may hold values from -6 to 6
- weight_bc: bfloat16 [2560, 256], replicated, may hold values from -0.015625 to 0.015625
- weight_dt: bfloat16 [2560, 40], replicated, may hold values from -0.125 to 0.125
- bias_dt: float32 [40], replicated, may hold values from -3 to 0.5
- log_rate: float32 [40], replicated, may hold values from -13.2 to -2.9
- skip_gain: float32 [40], replicated, may hold values from 0.5 to 1.5
- grad_out: bfloat16 [8192, 2560], P(('groups', 'seq')), parts along dimension 0, may hold values from -8 to 8
Outputs:
- grad_ssm_in: bfloat16 [8192, 2560], P(('groups', 'seq')), parts along dimension 0
- grad_layer_in: bfloat16 [8192, 2560], P(('groups', 'seq')), parts along dimension 0
- grad_weight_bc: float32 [5120, 256], P(('groups', 'seq')), parts along dimension 0
- grad_weight_dt: float32 [5120, 40], P(('groups', 'seq')), parts along dimension 0
- grad_bias_dt: float32 [80], P('groups'), parts along dimension 0
- grad_log_rate: float32 [80], P('groups'), parts along dimension 0
- grad_skip_gain: float32 [80], P('groups'), parts along dimension 0
There are 2 independent parts, one for each index of `groups`. A program takes and returns all parts, laid end to end along the dimension named above; an argument that names none is the same for every part. Nothing has to cross between parts.
All inputs are finite; a program needn't handle non-finite values.
Results may differ from a plain program's by a relative error of at most 0.0059.
Values sent between devices are 32-bit elements; how exact they have to be, the bound alone decides.
A program may use at most 128 MiB of HBM per device.

v0:
```python
import functools
import jax
import jax.numpy as jnp
from jax import lax
from jax.experimental import pallas as pl
from jax.experimental.pallas import tpu as pltpu
from jax.sharding import PartitionSpec as P

F32 = jnp.float32
BF16 = jnp.bfloat16
TILE = 128
CHUNKS = 4
VMEM_LIMIT = 60 * 1024 * 1024
VMEM = pl.BlockSpec(memory_space=pltpu.VMEM)


def mm(left, right):
    return lax.dot_general(left, right, (((1,), (0,)), ((), ())), preferred_element_type=F32)


def mm_nt(left, right):
    return lax.dot_general(left, right, (((1,), (1,)), ((), ())), preferred_element_type=F32)


def mm_tn(left, right):
    return lax.dot_general(left, right, (((0,), (0,)), ((), ())), preferred_element_type=F32)


def three_way(x):
    high = x.astype(BF16)
    rest = x - high.astype(F32)
    middle = rest.astype(BF16)
    return high, middle, (rest - middle.astype(F32)).astype(BF16)


def one_hot(heads, width, columns, first=0):
    row = lax.broadcasted_iota(jnp.int32, (heads, columns), 0)
    col = lax.broadcasted_iota(jnp.int32, (heads, columns), 1) + first
    inside = (col >= row * width) & (col < (row + 1) * width)
    return jnp.where(inside, 1.0, 0.0).astype(BF16)


def spread_heads(x, hot):
    parts = three_way(x)
    return mm(parts[0], hot) + mm(parts[1], hot) + mm(parts[2], hot)


def head_sum(x, hot):
    high = x.astype(BF16)
    low = (x - high.astype(F32)).astype(BF16)
    return mm_nt(high, hot) + mm_nt(low, hot)


def exact_mm(mask, x):
    parts = three_way(x)
    return mm(mask, parts[0]) + mm(mask, parts[1]) + mm(mask, parts[2])


def triangle(size, compare):
    row = lax.broadcasted_iota(jnp.int32, (size, size), 0)
    col = lax.broadcasted_iota(jnp.int32, (size, size), 1)
    return jnp.where(compare(row, col), 1.0, 0.0).astype(BF16)


def before_kernel(
    layer_ref, values_ref, wbc_ref, wdt_ref, bias_ref, rate_ref, grad_ref,
    proj_ref, raw_ref, run_ref, run_rows_ref, states_ref, total_ref, scores_ref, skip_ref,
    u_ref, runx_ref,
):
    tokens = layer_ref.shape[0]
    heads = bias_ref.shape[1]
    width = values_ref.shape[1]
    head_size = width // heads
    state_dim = wbc_ref.shape[1] // 2
    layer = layer_ref[...]
    proj = mm(layer, wbc_ref[...]).astype(BF16)
    proj_ref[...] = proj
    b_rows = proj[:, :state_dim]
    c_rows = proj[:, state_dim:]
    scores_ref[...] = mm_nt(b_rows, c_rows)
    raw = mm_nt(layer, wdt_ref[...]) + bias_ref[...]
    raw_ref[...] = raw
    step = jnp.maximum(raw, 0.0) + jnp.log1p(jnp.exp(-jnp.abs(raw)))
    decay = -jnp.exp(rate_ref[...]) * step
    run = exact_mm(triangle(tokens, lambda r, c: r >= c), decay)
    run_ref[...] = run
    run_rows = run.T
    for head in range(heads):
        run_rows_ref[head] = run_rows[head : head + 1]
    total = run[tokens - 1 :, :]
    total_ref[...] = jnp.zeros_like(total_ref)
    total_ref[:, :heads] = jnp.broadcast_to(total, (total_ref.shape[0], heads))
    hot = one_hot(heads, head_size, width)
    values = values_ref[...].astype(F32)
    grad = grad_ref[...].astype(F32)
    u_ref[...] = (spread_heads(step, hot) * values).astype(BF16)
    tail = spread_heads(jnp.exp(total - run) * step, hot)
    states_ref[0] = mm_tn(b_rows, (tail * values).astype(BF16))
    lead = spread_heads(jnp.exp(run), hot)
    states_ref[1] = mm_tn(c_rows, (lead * grad).astype(BF16))
    products = jnp.sum(values * grad, axis=0, keepdims=True)
    skip_ref[...] = head_sum(jnp.broadcast_to(products, (8, width)), hot)
    wide = one_hot(heads, TILE, heads * TILE)
    runx_ref[...] = spread_heads(run, wide)


def inner_pair(pair, u_ref, grad_ref, scores_ref, runx_ref, run_rows_ref,
               gu_ref, rows_ref, gscores_ref, head_size):
    tokens = u_ref.shape[0]
    blocks = tokens // TILE
    per = TILE // head_size
    cols = pl.ds(pl.multiple_of(pair * TILE, TILE), TILE)
    lane = lax.broadcasted_iota(jnp.int32, (TILE, TILE), 1)
    causal = lax.broadcasted_iota(jnp.int32, (TILE, TILE), 0) <= lane
    grads = [grad_ref[t * TILE : (t + 1) * TILE, cols] for t in range(blocks)]
    gus = [jnp.zeros((TILE, TILE), F32) for _ in range(blocks)]
    for sub in range(per):
        head = pair * per + sub
        keep = (lane >= sub * head_size) & (lane < (sub + 1) * head_size)
        hcols = pl.ds(pl.multiple_of(head * TILE, TILE), TILE)
        rows = [jnp.zeros((1, TILE), F32) for _ in range(blocks)]
        for s in range(blocks):
            srange = slice(s * TILE, (s + 1) * TILE)
            run_col = runx_ref[srange, hcols]
            u_head = jnp.where(keep, u_ref[srange, cols], jnp.zeros((), BF16))
            gu = jnp.zeros((TILE, TILE), F32)
            for t in range(s, blocks):
                trange = slice(t * TILE, (t + 1) * TILE)
                gap = run_rows_ref[head, :, trange] - run_col
                if s == t:
                    gap = jnp.where(causal, gap, -jnp.inf)
                factor = jnp.exp(gap)
                mixing = (factor * scores_ref[srange, trange]).astype(BF16)
                weight = mm_nt(u_head, grads[t])
                gscores_ref[srange, trange] += factor * weight
                rows[t] += jnp.sum(mixing.astype(F32) * weight, axis=0, keepdims=True)
                gu += mm(mixing, grads[t])
            gus[s] = jnp.where(keep, gu, gus[s])
        for t in range(blocks):
            rows_ref[head, :, t * TILE : (t + 1) * TILE] = rows[t]
    for s in range(blocks):
        gu_ref[s * TILE : (s + 1) * TILE, cols] = gus[s]


def scan_plan(devices, rows):
    levels = devices.bit_length() - 1
    sizes, halved = [rows], []
    for level in range(levels - 1):
        cut = sizes[-1] >= 16
        halved.append(cut)
        sizes.append(sizes[-1] // 2 if cut else sizes[-1])
    return levels, sizes, halved


def scan_kernel(devices, heads, states_ref, total_ref, u_ref, grad_ref, scores_ref, runx_ref,
                run_rows_ref, out_ref, gu_ref, rows_ref, gscores_ref, *refs):
    rows, width = states_ref.shape[1], states_ref.shape[2]
    head_size = width // heads
    levels, sizes, halved = scan_plan(devices, rows)
    top = levels - 1
    refs = list(refs)
    aggs = [states_ref] + [refs.pop(0) for _ in range(top)]
    gets = [refs.pop(0) for _ in range(top)]
    outs = [out_ref] + [refs.pop(0) for _ in range(top)]
    sends = [refs.pop(0) if halved[k] else None for k in range(top)]
    downs = [refs.pop(0) if halved[k] else None for k in range(top)]
    top_get, tots, tot_gets, decays, up_sems, down_sems, tot_sems = refs
    me = lax.axis_index("seq")
    bits = [lax.rem(me // (1 << k), 2) for k in range(levels)]
    partners = [me + (1 - 2 * bits[k]) * (1 << k) for k in range(levels)]
    barrier = pltpu.get_barrier_semaphore()
    for k in range(levels):
        pl.semaphore_signal(
            barrier, inc=1, device_id={"seq": partners[k]}, device_id_type=pl.DeviceIdType.MESH
        )
    pl.semaphore_wait(barrier, levels)
    span = width // CHUNKS

    def copy(source, target, send, receive, k):
        return pltpu.make_async_remote_copy(
            src_ref=source, dst_ref=target, send_sem=send, recv_sem=receive,
            device_id={"seq": partners[k]}, device_id_type=pl.DeviceIdType.MESH,
        )

    def half_at(k, which):
        size = sizes[k + 1]
        return pl.ds(pl.multiple_of(which * size, 8), size)

    def up_copy(k, c):
        cols = slice(c * span, (c + 1) * span)
        if k == top:
            source, target = aggs[k].at[bits[k], :, cols], top_get.at[:, cols]
        elif halved[k]:
            source, target = aggs[k].at[:, half_at(k, 1 - bits[k]), cols], gets[k].at[:, :, cols]
        else:
            source, target = aggs[k].at[:, :, cols], gets[k].at[:, :, cols]
        return copy(source, target, up_sems.at[0, k, c], up_sems.at[1, k, c], k)

    def down_copy(k, c):
        cols = slice(c * span, (c + 1) * span)
        return copy(sends[k].at[:, :, cols], downs[k].at[:, :, cols],
                    down_sems.at[0, k, c], down_sems.at[1, k, c], k)

    def tot_copy(k):
        return copy(tots.at[k], tot_gets.at[k], tot_sems.at[0, k], tot_sems.at[1, k], k)

    def tot_done(k):
        tot_copy(k).wait_recv()
        mine, other = tots[k], tot_gets[k]
        tots[k + 1] = mine + other
        left = jnp.where(bits[k] == 0, mine, other)
        right = jnp.where(bits[k] == 0, other, mine)
        hot = one_hot(TILE, head_size, width)
        decays[k, 0] = jnp.exp(spread_heads(left, hot))
        decays[k, 1] = jnp.exp(spread_heads(right, hot))

    def own(k, cols, part):
        if halved[k]:
            return aggs[k][part, half_at(k, bits[k]), cols]
        return aggs[k][part, :, cols]

    def finish_up(k, c):
        cols = slice(c * span, (c + 1) * span)
        up_copy(k, c).wait_recv()
        if c == 0:
            tot_done(k)
            if k + 1 < top:
                tot_copy(k + 1).start()
        first = bits[k] == 0
        s_mine, g_mine = own(k, cols, 0), own(k, cols, 1)
        s_got, g_got = gets[k][0, :, cols], gets[k][1, :, cols]
        s_left, s_right = jnp.where(first, s_mine, s_got), jnp.where(first, s_got, s_mine)
        g_left, g_right = jnp.where(first, g_mine, g_got), jnp.where(first, g_got, g_mine)
        aggs[k + 1][0, :, cols] = decays[k, 1, 0:1, cols] * s_left + s_right
        aggs[k + 1][1, :, cols] = g_left + decays[k, 0, 0:1, cols] * g_right
        up_copy(k + 1, c).start()

    def finish_top(c):
        cols = slice(c * span, (c + 1) * span)
        up_copy(top, c).wait_recv()
        got = top_get[:, cols]
        zero = jnp.zeros_like(got)
        outs[top][0, :, cols] = jnp.where(bits[top] == 1, got, zero)
        outs[top][1, :, cols] = jnp.where(bits[top] == 1, zero, got)
        if top > 0:
            step_down(top - 1, c)

    def step_down(k, c):
        cols = slice(c * span, (c + 1) * span)
        first = bits[k] == 0
        inc, outg = outs[k + 1][0, :, cols], outs[k + 1][1, :, cols]
        s_left = jnp.where(first, own(k, cols, 0), gets[k][0, :, cols])
        g_right = jnp.where(first, gets[k][1, :, cols], own(k, cols, 1))
        right_in = decays[k, 0, 0:1, cols] * inc + s_left
        left_out = decays[k, 1, 0:1, cols] * outg + g_right
        if halved[k]:
            sends[k][0, :, cols] = jnp.where(first, right_in, inc)
            sends[k][1, :, cols] = jnp.where(first, outg, left_out)
            down_copy(k, c).start()
            mine = half_at(k, bits[k])
        else:
            mine = slice(None)
        outs[k][0, mine, cols] = jnp.where(first, inc, right_in)
        outs[k][1, mine, cols] = jnp.where(first, left_out, outg)

    def finish_down(k, c):
        cols = slice(c * span, (c + 1) * span)
        if halved[k]:
            down_copy(k, c).wait_recv()
            outs[k][:, half_at(k, 1 - bits[k]), cols] = downs[k][:, :, cols]
        if k > 0:
            step_down(k - 1, c)

    tots[0] = total_ref[...]
    if top > 0:
        tot_copy(0).start()
    for c in range(CHUNKS):
        up_copy(0, c).start()
    stages = [functools.partial(finish_up, k) for k in range(top)]
    stages.append(finish_top)
    stages += [functools.partial(finish_down, k) for k in reversed(range(top))]
    gscores_ref[...] = jnp.zeros_like(gscores_ref)

    def body(pair, _):
        inner_pair(pair, u_ref, grad_ref, scores_ref, runx_ref, run_rows_ref,
                   gu_ref, rows_ref, gscores_ref, head_size)
        return 0

    pairs = width // TILE
    ticks = len(stages) + CHUNKS - 1
    for tick in range(ticks):
        lax.fori_loop(tick * pairs // ticks, (tick + 1) * pairs // ticks, body, 0)
        for c in range(CHUNKS):
            if 0 <= tick - c < len(stages):
                stages[tick - c](c)
    for k in range(top):
        tot_copy(k).wait_send()
    for c in range(CHUNKS):
        for k in range(levels):
            up_copy(k, c).wait_send()
        for k in range(top):
            if halved[k]:
                down_copy(k, c).wait_send()


def scan_states(devices, heads, states, total, u, grad, scores, runx, run_rows):
    rows, width = states.shape[1], states.shape[2]
    levels, sizes, halved = scan_plan(devices, rows)
    top = levels - 1
    scratch = [pltpu.VMEM((2, sizes[k + 1], width), F32) for k in range(top)]
    scratch += [pltpu.VMEM((2, sizes[k + 1], width), F32) for k in range(top)]
    scratch += [pltpu.VMEM((2, sizes[k + 1], width), F32) for k in range(top)]
    for _ in range(2):
        scratch += [pltpu.VMEM((2, sizes[k + 1], width), F32) for k in range(top) if halved[k]]
    scratch += [
        pltpu.VMEM((sizes[top], width), F32),
        pltpu.VMEM((levels + 1, 8, TILE), F32),
        pltpu.VMEM((levels, 8, TILE), F32),
        pltpu.VMEM((levels, 2, 8, width), F32),
        pltpu.SemaphoreType.DMA((2, levels, CHUNKS)),
        pltpu.SemaphoreType.DMA((2, levels, CHUNKS)),
        pltpu.SemaphoreType.DMA((2, levels)),
    ]
    return pl.pallas_call(
        functools.partial(scan_kernel, devices, heads),
        out_shape=[
            jax.ShapeDtypeStruct(shape, F32)
            for shape in (states.shape, u.shape, run_rows.shape, scores.shape)
        ],
        in_specs=[VMEM] * 7,
        out_specs=[VMEM] * 4,
        scratch_shapes=scratch,
        compiler_params=pltpu.CompilerParams(
            collective_id=0, has_side_effects=True, vmem_limit_bytes=VMEM_LIMIT
        ),
        name="scan_states",
    )(states, total, u, grad, scores, runx, run_rows)


def after_kernel(
    values_ref, grad_ref, proj_ref, raw_ref, run_ref, u_ref, rate_ref, skip_ref,
    gu_ref, rows_ref, gscores_ref, ends_ref, wbc_ref, wdt_ref, skip_sum_ref,
    gvalues_ref, glayer_ref, gproj_ref, small_ref,
):
    tokens, heads = raw_ref.shape
    width = values_ref.shape[1]
    head_size = width // heads
    state_dim = proj_ref.shape[1] // 2
    hot = one_hot(heads, head_size, width)
    raw, run = raw_ref[...], run_ref[...]
    rate = jnp.exp(rate_ref[...])
    step = jnp.maximum(raw, 0.0) + jnp.log1p(jnp.exp(-jnp.abs(raw)))
    total = run[tokens - 1 :, :]
    b_rows = proj_ref[:, :state_dim]
    c_rows = proj_ref[:, state_dim:]
    incoming, outgoing = ends_ref[0], ends_ref[1]
    inc_b, out_b = incoming.astype(BF16), outgoing.astype(BF16)
    values = values_ref[...].astype(F32)
    grad = grad_ref[...].astype(F32)
    step_wide = spread_heads(step, hot)
    lead_grad = spread_heads(jnp.exp(run), hot) * grad
    lead_b = lead_grad.astype(BF16)
    reads = head_sum(lead_grad * mm(c_rows, inc_b), hot)
    gscores = gscores_ref[...].astype(BF16)
    grad_c = mm_nt(lead_b, inc_b) + mm_tn(gscores, b_rows)
    tail_wide = spread_heads(jnp.exp(total - run), hot)
    back = tail_wide * mm(b_rows, out_b)
    grad_b = mm_nt((tail_wide * step_wide * values).astype(BF16), out_b) + mm(gscores, c_rows)
    gu = gu_ref[...]
    inner_cols = head_sum(u_ref[...].astype(F32) * gu, hot)
    back_sum = head_sum(values * back, hot)
    gu = gu + back
    gvalues_ref[...] = (step_wide * gu + spread_heads(skip_ref[...], hot) * grad).astype(BF16)
    grad_step = head_sum(values * gu, hot)
    cross = jnp.sum(incoming * outgoing, axis=0, keepdims=True)
    cross = head_sum(jnp.broadcast_to(cross, (8, width)), hot)[0:1]
    upper = triangle(tokens, lambda r, c: r <= c)
    lower = triangle(tokens, lambda r, c: r > c)
    inner = rows_ref[:, 0, :].T + reads - inner_cols
    grad_decay = exact_mm(upper, inner) + exact_mm(lower, step * back_sum) + jnp.exp(total) * cross
    sigmoid = 1.0 / (1.0 + jnp.exp(-raw))
    grad_raw = (grad_step - rate * grad_decay) * sigmoid
    gproj_ref[:, :state_dim] = grad_b.astype(BF16)
    gproj_ref[:, state_dim : 2 * state_dim] = grad_c.astype(BF16)
    gproj_ref[:, 2 * state_dim :] = grad_raw.astype(BF16)
    small_ref[...] = jnp.zeros_like(small_ref)
    small_ref[0:1, :heads] = jnp.sum(grad_raw, axis=0, keepdims=True)
    small_ref[1:2, :heads] = -rate * jnp.sum(grad_decay * step, axis=0, keepdims=True)
    small_ref[2:3, :heads] = skip_sum_ref[0:1]
    glayer_ref[...] = (
        mm_nt(gproj_ref[:, : 2 * state_dim], wbc_ref[...])
        + mm(grad_raw.astype(BF16), wdt_ref[...])
    ).astype(BF16)


def packing(depth, devices, heads):
    share = depth // devices
    lanes = TILE // heads
    group = -(-share // (8 * lanes)) * 8
    return share, lanes, group


def reduce_kernel(devices, heads, layer_ref, gproj_ref, small_ref,
                  gbc_ref, gdt_ref, gbias_ref, grate_ref, gskip_ref, *refs):
    depth = layer_ref.shape[1]
    share, lanes, group = packing(depth, devices, heads)
    levels = devices.bit_length() - 1
    wide = gbc_ref.shape[1]
    planes = wide // TILE + 1
    refs = list(refs)
    sems = refs.pop()
    sums = [refs.pop(0) for _ in range(planes)]
    gets = [[refs.pop(0) for _ in range(levels)] for _ in range(planes)]
    units = [share] * (planes - 1) + [group + 8]
    me = lax.axis_index("seq")
    bits = [lax.rem(me // (1 << k), 2) for k in range(levels)]
    partners = [me + (1 - 2 * bits[k]) * (1 << k) for k in range(levels)]
    offsets = [0]
    for k in range(levels):
        offsets.append(offsets[k] + bits[k] * (devices >> (k + 1)))
    barrier = pltpu.get_barrier_semaphore()
    for k in range(levels):
        pl.semaphore_signal(
            barrier, inc=1, device_id={"seq": partners[k]}, device_id_type=pl.DeviceIdType.MESH
        )
    pl.semaphore_wait(barrier, levels)
    places = [
        sum(((shard >> k) & 1) * (devices >> (k + 1)) for k in range(levels))
        for shard in range(devices)
    ]

    def half(k, plane, which):
        size = (devices >> (k + 1)) * units[plane]
        start = (offsets[k] + which * (devices >> (k + 1))) * units[plane]
        return pl.ds(pl.multiple_of(start, 8), size)

    def copy(k, plane):
        return pltpu.make_async_remote_copy(
            src_ref=sums[plane].at[half(k, plane, 1 - bits[k])],
            dst_ref=gets[plane][k],
            send_sem=sems.at[0, k, plane],
            recv_sem=sems.at[1, k, plane],
            device_id={"seq": partners[k]},
            device_id_type=pl.DeviceIdType.MESH,
        )

    layer = layer_ref[...]
    rows_bc = mm_tn(layer, gproj_ref[:, :wide])
    for plane in range(planes - 1):
        for shard in range(devices):
            sums[plane][places[shard] * share : (places[shard] + 1) * share] = rows_bc[
                shard * share : (shard + 1) * share, plane * TILE : (plane + 1) * TILE
            ]
        copy(0, plane).start()
    row = lax.broadcasted_iota(jnp.int32, (heads, lanes * TILE), 0)
    col = lax.broadcasted_iota(jnp.int32, (heads, lanes * TILE), 1)
    shift = jnp.zeros(row.shape, F32)
    for j in range(lanes):
        shift = jnp.where(col == row + j * (TILE + heads), 1.0, shift)
    moved = mm(gproj_ref[:, wide:], shift.astype(BF16)).astype(BF16)
    rows_dt = mm_tn(layer, moved)
    unit = group + 8
    for shard in range(devices):
        start = places[shard] * unit
        packed = jnp.zeros((group, TILE), F32)
        for j in range(lanes):
            count = min(share - j * group, group)
            if count <= 0:
                continue
            part = rows_dt[
                shard * share + j * group : shard * share + j * group + count,
                j * TILE : (j + 1) * TILE,
            ]
            if count < group:
                part = jnp.concatenate([part, jnp.zeros((group - count, TILE), F32)], axis=0)
            packed = packed + part
        sums[-1][start : start + group] = packed
        sums[-1][start + group : start + unit] = small_ref[...]
    copy(0, planes - 1).start()

    for tick in range(levels + planes - 1):
        for plane in range(planes):
            k = tick - plane
            if not 0 <= k < levels:
                continue
            copy(k, plane).wait_recv()
            mine = half(k, plane, bits[k])
            sums[plane][mine] = sums[plane][mine] + gets[plane][k][...]
            if k + 1 < levels:
                copy(k + 1, plane).start()
    for plane in range(planes - 1):
        start = pl.multiple_of(offsets[levels] * share, 8)
        gbc_ref[:, plane * TILE : (plane + 1) * TILE] = sums[plane][pl.ds(start, share)]
    last = sums[-1][pl.ds(pl.multiple_of(offsets[levels] * unit, 8), unit)]
    for j in range(lanes):
        count = min(share - j * group, group)
        if count > 0:
            gdt_ref[j * group : j * group + count] = last[:count, j * heads : (j + 1) * heads]
    gbias_ref[...] = last[group : group + 1, :heads]
    grate_ref[...] = last[group + 1 : group + 2, :heads]
    gskip_ref[...] = last[group + 2 : group + 3, :heads]
    for plane in range(planes):
        for k in range(levels):
            copy(k, plane).wait_send()


def reduce_rows(devices, heads, layer_in, grad_proj, small):
    depth = layer_in.shape[1]
    wide = grad_proj.shape[1] - heads
    share, lanes, group = packing(depth, devices, heads)
    levels = devices.bit_length() - 1
    units = [share] * (wide // TILE) + [group + 8]
    scratch = [pltpu.VMEM((devices * unit, TILE), F32) for unit in units]
    for unit in units:
        scratch += [pltpu.VMEM(((devices >> (k + 1)) * unit, TILE), F32) for k in range(levels)]
    scratch.append(pltpu.SemaphoreType.DMA((2, levels, len(units))))
    shapes = [(share, wide), (share, heads), (1, heads), (1, heads), (1, heads)]
    return pl.pallas_call(
        functools.partial(reduce_kernel, devices, heads),
        out_shape=[jax.ShapeDtypeStruct(shape, F32) for shape in shapes],
        in_specs=[VMEM] * 3,
        out_specs=[VMEM] * 5,
        scratch_shapes=scratch,
        compiler_params=pltpu.CompilerParams(
            collective_id=1, has_side_effects=True, vmem_limit_bytes=VMEM_LIMIT
        ),
        name="reduce_rows",
    )(layer_in, grad_proj, small)


def call(kernel, shapes, name, *operands):
    return pl.pallas_call(
        kernel,
        out_shape=[jax.ShapeDtypeStruct(shape, dtype) for shape, dtype in shapes],
        in_specs=[VMEM] * len(operands),
        out_specs=[VMEM] * len(shapes),
        compiler_params=pltpu.CompilerParams(vmem_limit_bytes=VMEM_LIMIT),
        name=name,
    )(*operands)


def local(layer_in, ssm_in, weight_bc, weight_dt, bias_dt, log_rate, skip_gain, grad_out):
    tokens, depth = layer_in.shape
    heads = log_rate.shape[0]
    width = ssm_in.shape[1]
    state_dim = weight_bc.shape[1] // 2
    head_size = width // heads
    devices = lax.axis_size("seq")
    narrow = weight_dt.T
    bias, rate, gain = bias_dt[None, :], log_rate[None, :], skip_gain[None, :]
    proj, raw, run, run_rows, states, total, scores, skip_sum, u, runx = call(
        before_kernel,
        [
            ((tokens, 2 * state_dim), BF16),
            ((tokens, heads), F32),
            ((tokens, heads), F32),
            ((heads, 1, tokens), F32),
            ((2, state_dim, width), F32),
            ((8, TILE), F32),
            ((tokens, tokens), F32),
            ((8, heads), F32),
            ((tokens, width), BF16),
            ((tokens, heads * TILE), F32),
        ],
        "before",
        layer_in, ssm_in, weight_bc, narrow, bias, rate, grad_out,
    )
    ends, gu, rows, gscores = scan_states(
        devices, heads, states, total, u, grad_out, scores, runx, run_rows
    )
    grad_ssm_in, grad_layer_in, grad_proj, small = call(
        after_kernel,
        [
            ((tokens, width), BF16),
            ((tokens, depth), BF16),
            ((tokens, 2 * state_dim + heads), BF16),
            ((8, TILE), F32),
        ],
        "after",
        ssm_in, grad_out, proj, raw, run, u, rate, gain, gu, rows, gscores, ends,
        weight_bc, narrow, skip_sum,
    )
    grad_bc, grad_dt, grad_bias, grad_rate, grad_skip = reduce_rows(
        devices, heads, layer_in, grad_proj, small
    )
    return (
        grad_ssm_in,
        grad_layer_in,
        grad_bc,
        grad_dt,
        grad_bias[0],
        grad_rate[0],
        grad_skip[0],
    )


def solution(mesh):
    rows = P(("groups", "seq"), None)
    in_specs = (rows, rows, P(), P(), P(), P(), P(), rows)
    out_specs = (rows, rows, rows, rows, P("groups"), P("groups"), P("groups"))
    return jax.shard_map(local, mesh=mesh, in_specs=in_specs, out_specs=out_specs, check_vma=False)
```

profile of v0, /device:TPU:0, one launch (start us, length us, event | category | flops | bytes accessed | tf_op | source)
XLA Modules:
  0.0 128.0 jit_solution(9145243835186657560)
XLA Ops:
  0.6 13.2 %before.1 = (bf16[256,256]{1,0:T(8,128)(2,1)}, f32[256,40]{1,0:T(8,128)}, f32[256,40]{1,0:T(8,128)}, f32[40,1,256]{2,1,0:T(1,128)}, f32[2,128,2560]{2,1,0:T(8,12...) custom-call(bf16[256,2560]{1,0:T(8,128)(2,1)} %layer_ref.3, ...), custom_call_target="tpu_custom_call" | custom-call | tf_op jit(solution)/shard_map/before/pallas_call | solution.py:532
  13.9 54.5 %scan_states.1 = (f32[2,128,2560]{2,1,0:T(8,128)}, f32[256,2560]{1,0:T(8,128)}, f32[40,1,256]{2,1,0:T(1,128)}, f32[256,256]{1,0:T(8,128)}) custom-call(f32[2,128,2560]{2,1,0:T(8,128)} %get-tuple-element.34.states_ref, f32[8,128]{1,0:T(8,128)} %get-tuple-element.35.total_ref, bf16[256,2560]{1,0:T(8,128)(2,1)} %get-tuple-element.33.u_ref, ...), custom_call_target="tpu_custom_call" | custom-call | tf_op jit(solution)/shard_map/scan_states/pallas_call | solution.py:324
  68.4 16.2 %after.1 = (bf16[256,2560]{1,0:T(8,128)(2,1)}, bf16[256,2560]{1,0:T(8,128)(2,1)}, bf16[256,296]{1,0:T(8,128)(2,1)}, f32[8,128]{1,0:T(8,128)}) custom-call(bf16[256,2560]{1,0:T(8,128)(2,1)} %values_ref.3, bf16[256,2560]{1,0:T(8,128)(2,1)} %grad_ref.5, bf16[256,256]{1,0:T(8,128)(2,1)} %get-tuple-element.30.proj_ref, f32[256,40]{1,0:T(8,128)} %get-tuple-element.31.raw_ref, ...), custom_call_target="tpu_custom_call" | custom-call | tf_op jit(solution)/shard_map/after/pallas_call | solution.py:532
  84.6 36.7 %reduce_rows.1 = (f32[160,256]{1,0:T(8,128)}, f32[160,40]{1,0:T(8,128)}, f32[1,40]{1,0:T(1,128)}, f32[1,40]{1,0:T(1,128)}, f32[1,40]{1,0:T(1,128)}) custom-call(bf16[256,2560]{1,0:T(8,128)(2,1)} %layer_ref.3, bf16[256,296]{1,0:T(8,128)(2,1)} %get-tuple-element.46.gproj_ref, f32[8,128]{1,0:T(8,128)} %get-tuple-element.47.small_ref), custom_call_target="tpu_custom_call" | custom-call | tf_op jit(solution)/shard_map/reduce_rows/pallas_call | solution.py:518
  121.4 1.6 %copy.15 = f32[160,40]{0,1:T(8,128)} copy(f32[160,40]{1,0:T(8,128)} %get-tuple-element.56) | data formatting | bytes 51200
  122.9 1.6 %copy.20 = f32[160,256]{1,0:T(8,128)} copy(f32[160,256]{1,0:T(8,128)} %get-tuple-element.69) | data formatting | bytes 327680
  124.5 1.2 copy.21
  125.7 1.2 copy.22
  126.9 1.1 copy.23
where the time goes:
time: 128 us
  Pallas kernels  121 us (95%)
  local copies, waits for them, and re-layouts  6.66 us (5%)
    pallas_call x1, Pallas kernels, scan_states(): pl.pallas_call(functools.partial(scan_kernel, devices, heads), out_shape=...  54.5 us
    pallas_call x1, Pallas kernels, reduce_rows(): pl.pallas_call(functools.partial(reduce_kernel, devices, heads), out_shap...  36.7 us
    pallas_call x2, Pallas kernels, call(): pl.pallas_call(kernel, out_shape=[jax.ShapeDtypeStruct(shape, dtype) for...  29.4 us
    unnamed x5, local copies, waits for them, and re-layouts  6.66 us

commit v1 on v0

v1 whole, which is shorter than its diff:
```python
import functools
import jax
import jax.numpy as jnp
from jax import lax
from jax.experimental import pallas as pl
from jax.experimental.pallas import tpu as pltpu
from jax.sharding import PartitionSpec as P

F32 = jnp.float32
BF16 = jnp.bfloat16
TILE = 128
CHUNKS = 5
VMEM_LIMIT = 60 * 1024 * 1024
VMEM = pl.BlockSpec(memory_space=pltpu.VMEM)
ANY = pl.BlockSpec(memory_space=pl.ANY)


def mm(left, right):
    return lax.dot_general(left, right, (((1,), (0,)), ((), ())), preferred_element_type=F32)


def mm_nt(left, right):
    return lax.dot_general(left, right, (((1,), (1,)), ((), ())), preferred_element_type=F32)


def mm_tn(left, right):
    return lax.dot_general(left, right, (((0,), (0,)), ((), ())), preferred_element_type=F32)


def three_way(x):
    high = x.astype(BF16)
    rest = x - high.astype(F32)
    middle = rest.astype(BF16)
    return high, middle, (rest - middle.astype(F32)).astype(BF16)


def one_hot(heads, width, columns, first=0):
    row = lax.broadcasted_iota(jnp.int32, (heads, columns), 0)
    col = lax.broadcasted_iota(jnp.int32, (heads, columns), 1) + first
    inside = (col >= row * width) & (col < (row + 1) * width)
    return jnp.where(inside, 1.0, 0.0).astype(BF16)


def spread(parts, hot):
    return mm(parts[0], hot) + mm(parts[1], hot) + mm(parts[2], hot)


def head_sum(x, hot):
    high = x.astype(BF16)
    low = (x - high.astype(F32)).astype(BF16)
    return mm_nt(high, hot) + mm_nt(low, hot)


def exact_mm(mask, x):
    parts = three_way(x)
    return mm(mask, parts[0]) + mm(mask, parts[1]) + mm(mask, parts[2])


def triangle(size, compare):
    row = lax.broadcasted_iota(jnp.int32, (size, size), 0)
    col = lax.broadcasted_iota(jnp.int32, (size, size), 1)
    return jnp.where(compare(row, col), 1.0, 0.0).astype(BF16)


def inner_pair(pair, heads, u_ref, grad_ref, scores_ref, parts_ref, run_rows_ref,
               gu_ref, rows_ref, gscores_ref, head_size):
    tokens = u_ref.shape[0]
    blocks = tokens // TILE
    per = TILE // head_size
    cols = pl.ds(pl.multiple_of(pair * TILE, TILE), TILE)
    lane = lax.broadcasted_iota(jnp.int32, (TILE, TILE), 1)
    causal = lax.broadcasted_iota(jnp.int32, (TILE, TILE), 0) <= lane
    wide = one_hot(heads, TILE, per * TILE, pair * (per * TILE))
    run_cols = spread([parts_ref[i] for i in range(3)], wide)
    grads = [grad_ref[t * TILE : (t + 1) * TILE, cols] for t in range(blocks)]
    gus = [jnp.zeros((TILE, TILE), F32) for _ in range(blocks)]
    for sub in range(per):
        head = pair * per + sub
        keep = (lane >= sub * head_size) & (lane < (sub + 1) * head_size)
        rows = [jnp.zeros((1, TILE), F32) for _ in range(blocks)]
        for s in range(blocks):
            srange = slice(s * TILE, (s + 1) * TILE)
            run_col = run_cols[srange, sub * TILE : (sub + 1) * TILE]
            u_head = jnp.where(keep, u_ref[srange, cols], jnp.zeros((), BF16))
            gu = jnp.zeros((TILE, TILE), F32)
            for t in range(s, blocks):
                trange = slice(t * TILE, (t + 1) * TILE)
                gap = run_rows_ref[head, :, trange] - run_col
                if s == t:
                    gap = jnp.where(causal, gap, -jnp.inf)
                factor = jnp.exp(gap)
                mixing = (factor * scores_ref[srange, trange]).astype(BF16)
                weight = mm_nt(u_head, grads[t])
                gscores_ref[srange, trange] += factor * weight
                rows[t] += jnp.sum(mixing.astype(F32) * weight, axis=0, keepdims=True)
                gu += mm(mixing, grads[t])
            gus[s] = jnp.where(keep, gu, gus[s])
        for t in range(blocks):
            rows_ref[head, :, t * TILE : (t + 1) * TILE] = rows[t]
    for s in range(blocks):
        gu_ref[s * TILE : (s + 1) * TILE, cols] = gus[s]


def packing(depth, devices, heads):
    share = depth // devices
    lanes = TILE // heads
    group = -(-share // (8 * lanes)) * 8
    return share, lanes, group


def reduce_plan(depth, devices, heads):
    share, lanes, group = packing(depth, devices, heads)
    levels = devices.bit_length() - 1
    y_first = list(range(levels))
    z_first = [0] + list(range(2, levels)) + [1]
    pieces = 2 if share % 32 == 0 else 1
    plan = []
    for plane, order in ((1, z_first), (0, y_first)):
        for piece in range(pieces):
            size = share // pieces
            plan.append((plane, piece * size, size, order))
    plan.append((2, 0, group + 8, y_first))
    return plan


def scratch_list(tokens, depth, width, heads, state_dim, devices):
    levels = devices.bit_length() - 1
    half, quarter = state_dim // 2, state_dim // 4
    plan = reduce_plan(depth, devices, heads)
    names = {}

    def add(name, shape, dtype=F32):
        names[name] = pltpu.VMEM(shape, dtype)

    add("layer", (tokens, depth), BF16)
    add("values", (tokens, width), BF16)
    add("grad", (tokens, width), BF16)
    add("wbc", (depth, 2 * state_dim), BF16)
    add("wdt", (heads, depth), BF16)
    add("layer_t", (depth, tokens), BF16)
    add("proj", (tokens, 2 * state_dim), BF16)
    add("proj_t", (2 * state_dim, tokens), BF16)
    add("hot", (TILE, width), BF16)
    add("parts", (3, tokens, heads), BF16)
    for name in ("raw", "step", "run"):
        add(name, (tokens, heads))
    add("run_rows", (heads, 1, tokens))
    add("rows", (heads, 1, tokens))
    add("scores", (tokens, tokens))
    add("gscores", (tokens, tokens))
    for name in ("step_w", "lead_w", "tail_w", "gu"):
        add(name, (tokens, width))
    for name in ("u", "tsv", "lg"):
        add(name, (tokens, width), BF16)
    for name in ("reads", "cols", "backs", "gsteps"):
        add(name, (tokens, heads))
    add("cross", (8, heads))
    add("skips", (8, heads))
    add("gc", (tokens, state_dim))
    add("gb", (tokens, state_dim))
    add("gproj", (tokens, 2 * state_dim + heads), BF16)
    add("gvalues", (tokens, width), BF16)
    add("glayer", (tokens, depth), BF16)
    for kind in ("s", "g"):
        add("st_" + kind, (state_dim, width))
        add("get0_" + kind, (half, width))
        add("agg1_" + kind, (half, width))
        add("get1_" + kind, (quarter, width))
        add("agg2_" + kind, (quarter, width))
        add("zin_" + kind, (quarter, width))
        add("zout_" + kind, (quarter, width))
        add("send1_" + kind, (quarter, width))
        add("chip_" + kind, (half, width))
        add("send0_" + kind, (half, width))
        add("end_" + kind, (state_dim, width))
    add("tots", (2, 8, TILE))
    add("tot_gets", (2, 8, TILE))
    add("decays", (5, 8, width))
    for q, (plane, first, size, order) in enumerate(plan):
        add(f"sum{q}", (devices * size, TILE))
        for i in range(levels):
            add(f"rget{q}_{i}", ((devices >> (i + 1)) * size, TILE))
    add_sem = lambda name, shape: names.__setitem__(name, pltpu.SemaphoreType.DMA(shape))
    add_sem("load", (5,))
    add_sem("store", (2,))
    add_sem("comm", (2, 5, 2, CHUNKS))
    add_sem("tot_sems", (2, 2))
    add_sem("rsem", (2, levels, len(plan)))
    return names


class Box:
    pass


def mega_kernel(devices, names, layer_hbm, values_hbm, wbc_hbm, wdt_hbm, bias_ref, rate_ref,
                gain_ref, grad_hbm, gvalues_hbm, glayer_hbm, gbc_ref, last_ref, *refs):
    r = Box()
    for name, ref in zip(names, refs):
        setattr(r, name, ref)
    tokens, depth = r.layer.shape
    width = r.values.shape[1]
    heads = bias_ref.shape[1]
    head_size = width // heads
    state_dim = r.st_s.shape[0]
    half, quarter = state_dim // 2, state_dim // 4
    levels = devices.bit_length() - 1
    zrows = devices // 4
    span = width // CHUNKS
    me = lax.axis_index("seq")
    bits = [lax.rem(me // (1 << k), 2) for k in range(levels)]
    partners = [me + (1 - 2 * bits[k]) * (1 << k) for k in range(levels)]
    row = me // 4
    up_row = lax.rem(me + 4, devices)
    down_row = lax.rem(me + devices - 4, devices)
    mesh_id = pl.DeviceIdType.MESH

    loads = [
        pltpu.make_async_copy(source, target, r.load.at[i])
        for i, (source, target) in enumerate((
            (layer_hbm, r.layer), (wbc_hbm, r.wbc), (wdt_hbm, r.wdt),
            (values_hbm, r.values), (grad_hbm, r.grad),
        ))
    ]
    for load in loads:
        load.start()

    barrier = pltpu.get_barrier_semaphore()
    for k in range(levels):
        pl.semaphore_signal(barrier, inc=1, device_id={"seq": partners[k]}, device_id_type=mesh_id)
    if zrows > 1:
        @pl.when(row < zrows - 1)
        def _():
            pl.semaphore_signal(barrier, inc=1, device_id={"seq": up_row}, device_id_type=mesh_id)

        @pl.when(row > 0)
        def _():
            pl.semaphore_signal(barrier, inc=1, device_id={"seq": down_row}, device_id_type=mesh_id)

    r.hot[...] = one_hot(TILE, head_size, width)
    loads[0].wait()
    loads[1].wait()
    layer = r.layer[...]
    proj = mm(layer, r.wbc[...]).astype(BF16)
    r.proj[...] = proj
    r.proj_t[...] = proj.T
    loads[2].wait()
    raw = mm_nt(layer, r.wdt[...]) + bias_ref[...]
    r.raw[...] = raw
    step = jnp.maximum(raw, 0.0) + jnp.log1p(jnp.exp(-jnp.abs(raw)))
    r.step[...] = step
    decay = -jnp.exp(rate_ref[...]) * step
    run = exact_mm(triangle(tokens, lambda a, b: a >= b), decay)
    r.run[...] = run
    total = run[tokens - 1 :, :]
    r.tots[0] = jnp.zeros((8, TILE), F32)
    r.tots[0, :, :heads] = jnp.broadcast_to(total, (8, heads))
    if zrows > 1:
        count = levels + jnp.where(row < zrows - 1, 1, 0) + jnp.where(row > 0, 1, 0)
    else:
        count = levels
    pl.semaphore_wait(barrier, count)

    def remote(source, target, send, receive, device):
        return pltpu.make_async_remote_copy(
            src_ref=source, dst_ref=target, send_sem=send, recv_sem=receive,
            device_id={"seq": device}, device_id_type=mesh_id,
        )

    def tot_copy(k):
        return remote(r.tots.at[k], r.tot_gets.at[k], r.tot_sems.at[0, k], r.tot_sems.at[1, k],
                      partners[k])

    tot_copy(0).start()

    kinds = ("s", "g")

    def cols_of(k):
        return slice(k * span, (k + 1) * span)

    def at(name, kind):
        return getattr(r, name + "_" + kind)

    def rows_at(which, size):
        return pl.ds(pl.multiple_of(which * size, 8), size)

    def copy(stage, kind, k):
        cols = cols_of(k)
        if stage == 0:
            source = at("st", kind).at[rows_at(1 - bits[0], half), cols]
            target, device = at("get0", kind).at[:, cols], partners[0]
        elif stage == 1:
            source = at("agg1", kind).at[rows_at(1 - bits[1], quarter), cols]
            target, device = at("get1", kind).at[:, cols], partners[1]
        elif stage == 2:
            source, target = at("zout", kind).at[:, cols], at("zin", kind).at[:, cols]
            device = up_row if kind == "s" else down_row
        elif stage == 3:
            source = at("send1", kind).at[:, cols]
            target, device = at("chip", kind).at[rows_at(bits[1], quarter), cols], partners[1]
        else:
            source = at("send0", kind).at[:, cols]
            target, device = at("end", kind).at[rows_at(bits[0], half), cols], partners[0]
        i = kinds.index(kind)
        return remote(source, target, r.comm.at[0, stage, i, k], r.comm.at[1, stage, i, k], device)

    def tot_done(k):
        tot_copy(k).wait_recv()
        mine, other = r.tots[k], r.tot_gets[k]
        both = jnp.concatenate([mine, other], axis=0)
        stacked = jnp.concatenate(list(three_way(both)), axis=0)
        wide = mm(stacked, r.hot[...])
        wide = jnp.exp(wide[0:16] + wide[16:32] + wide[32:48])
        r.decays[2 * k] = wide[0:8]
        r.decays[2 * k + 1] = wide[8:16]
        if k == 0:
            r.tots[1] = mine + other
            tot_copy(1).start()
        else:
            r.decays[4] = wide[0:8] * wide[8:16]

    first0, first1 = bits[0] == 0, bits[1] == 0

    def make_states(kind, k):
        if k == 0:
            loads[3 if kind == "s" else 4].wait()
        cols = cols_of(k)
        hot = r.hot[:heads, cols]
        if kind == "s":
            step_w = spread(three_way(r.step[...]), hot)
            r.step_w[:, cols] = step_w
            run = r.run[...]
            tail_w = spread(three_way(jnp.exp(run[tokens - 1 :, :] - run)), hot)
            r.tail_w[:, cols] = tail_w
            u = step_w * r.values[:, cols].astype(F32)
            r.u[:, cols] = u.astype(BF16)
            tsv = (tail_w * u).astype(BF16)
            r.tsv[:, cols] = tsv
            r.st_s[:, cols] = mm(r.proj_t[:state_dim], tsv)
        else:
            lead_w = spread(three_way(jnp.exp(r.run[...])), hot)
            r.lead_w[:, cols] = lead_w
            lg = (lead_w * r.grad[:, cols].astype(F32)).astype(BF16)
            r.lg[:, cols] = lg
            r.st_g[:, cols] = mm(r.proj_t[state_dim:], lg)
        copy(0, kind, k).start()

    def merge(kind, first, mine, got, e_mine, e_other):
        if kind == "s":
            return jnp.where(first, e_other * mine + got, mine + e_mine * got)
        return jnp.where(first, mine + e_mine * got, e_other * mine + got)

    def split(kind, first, parent, mine, got, e_mine, e_other):
        far, near = e_other * parent + got, e_mine * parent + mine
        if kind == "s":
            return jnp.where(first, parent, far), jnp.where(first, near, parent)
        return jnp.where(first, far, parent), jnp.where(first, parent, near)

    def pair_up(kind, k):
        if kind == "s" and k == 0:
            tot_done(0)
        copy(0, kind, k).wait_recv()
        cols = cols_of(k)
        mine = at("st", kind)[rows_at(bits[0], half), cols]
        got = at("get0", kind)[:, cols]
        at("agg1", kind)[:, cols] = merge(
            kind, first0, mine, got, r.decays[0, 0:1, cols], r.decays[1, 0:1, cols])
        copy(1, kind, k).start()

    def row_up(kind, k):
        if kind == "s" and k == 0:
            tot_done(1)
        copy(1, kind, k).wait_recv()
        cols = cols_of(k)
        mine = at("agg1", kind)[rows_at(bits[1], quarter), cols]
        got = at("get1", kind)[:, cols]
        at("agg2", kind)[:, cols] = merge(
            kind, first1, mine, got, r.decays[2, 0:1, cols], r.decays[3, 0:1, cols])

    def chain(kind, k, place):
        cols = cols_of(k)
        if place > 0:
            copy(2, kind, k).wait_recv()
            parent = at("zin", kind)[:, cols]
        else:
            parent = jnp.zeros((quarter, span), F32)
        if place < zrows - 1:
            passed = at("agg2", kind)[:, cols]
            if place > 0:
                passed = r.decays[4, 0:1, cols] * parent + passed
            at("zout", kind)[:, cols] = passed
            copy(2, kind, k).start()
        mine = at("agg1", kind)[rows_at(bits[1], quarter), cols]
        got = at("get1", kind)[:, cols]
        kept, sent = split(kind, first1, parent, mine, got,
                           r.decays[2, 0:1, cols], r.decays[3, 0:1, cols])
        at("send1", kind)[:, cols] = sent
        copy(3, kind, k).start()
        at("chip", kind)[rows_at(bits[1], quarter), cols] = kept

    def chain_slot(kind, k, place):
        where = place if kind == "s" else zrows - 1 - place
        if zrows == 1:
            chain(kind, k, place)
        else:
            pl.when(row == where)(lambda: chain(kind, k, place))

    def chip_down(kind, k):
        copy(3, kind, k).wait_recv()
        cols = cols_of(k)
        parent = at("chip", kind)[:, cols]
        mine = at("st", kind)[rows_at(bits[0], half), cols]
        got = at("get0", kind)[:, cols]
        kept, sent = split(kind, first0, parent, mine, got,
                           r.decays[0, 0:1, cols], r.decays[1, 0:1, cols])
        at("send0", kind)[:, cols] = sent
        copy(4, kind, k).start()
        at("end", kind)[rows_at(bits[0], half), cols] = kept

    def gather(name, k, x):
        ref = getattr(r, name)
        ref[...] = x if k == 0 else ref[...] + x

    def forward_tail(k):
        copy(4, "s", k).wait_recv()
        cols = cols_of(k)
        hot = r.hot[:heads, cols]
        inc = r.end_s[:, cols].astype(BF16)
        lead_grad = r.lead_w[:, cols] * r.grad[:, cols].astype(F32)
        gather("reads", k, head_sum(lead_grad * mm(r.proj[:, state_dim:], inc), hot))
        gather("gc", k, mm_nt(r.lg[:, cols], inc))

    def inner_tail(k):
        cols = cols_of(k)
        hot = r.hot[:heads, cols]
        gather("cols", k, head_sum(r.u[:, cols].astype(F32) * r.gu[:, cols], hot))
        products = r.values[:, cols].astype(F32) * r.grad[:, cols].astype(F32)
        products = jnp.sum(products, axis=0, keepdims=True)
        gather("skips", k, head_sum(jnp.broadcast_to(products, (8, span)), hot))

    def backward_tail(k):
        copy(4, "g", k).wait_recv()
        cols = cols_of(k)
        hot = r.hot[:heads, cols]
        outgoing = r.end_g[:, cols]
        out = outgoing.astype(BF16)
        values = r.values[:, cols].astype(F32)
        gather("gb", k, mm_nt(r.tsv[:, cols], out))
        back = r.tail_w[:, cols] * mm(r.proj[:, :state_dim], out)
        gather("backs", k, head_sum(values * back, hot))
        gu = r.gu[:, cols] + back
        gather("gsteps", k, head_sum(values * gu, hot))
        cross = jnp.sum(r.end_s[:, cols] * outgoing, axis=0, keepdims=True)
        gather("cross", k, head_sum(jnp.broadcast_to(cross, (8, span)), hot))
        gain = spread(three_way(jnp.broadcast_to(gain_ref[...], (8, heads))), hot)[0:1]
        r.gvalues[:, cols] = (
            r.step_w[:, cols] * gu + gain * r.grad[:, cols].astype(F32)
        ).astype(BF16)

    plan = reduce_plan(depth, devices, heads)
    share, lanes, group = packing(depth, devices, heads)

    def places(order):
        return [
            sum(((shard >> order[i]) & 1) * (devices >> (i + 1)) for i in range(levels))
            for shard in range(devices)
        ]

    def offset(order, count):
        result = 0
        for i in range(count):
            result = result + bits[order[i]] * (devices >> (i + 1))
        return result

    def part(q, i, which):
        size, order = plan[q][2], plan[q][3]
        start = (offset(order, i) + which * (devices >> (i + 1))) * size
        return pl.ds(pl.multiple_of(start, 8), (devices >> (i + 1)) * size)

    def reduce_copy(q, i):
        k = plan[q][3][i]
        return remote(
            getattr(r, f"sum{q}").at[part(q, i, 1 - bits[k])], getattr(r, f"rget{q}_{i}"),
            r.rsem.at[0, i, q], r.rsem.at[1, i, q], partners[k],
        )

    def reduce_step(q, i):
        k = plan[q][3][i]
        reduce_copy(q, i).wait_recv()
        sums = getattr(r, f"sum{q}")
        mine = part(q, i, bits[k])
        sums[mine] = sums[mine] + getattr(r, f"rget{q}_{i}")[...]
        if i + 1 < levels:
            reduce_copy(q, i + 1).start()

    def plane_start(plane, product):
        for q, (owner, first, size, order) in enumerate(plan):
            if owner != plane:
                continue
            sums = getattr(r, f"sum{q}")
            where = places(order)
            for shard in range(devices):
                start = shard * share + first
                sums[where[shard] * size : (where[shard] + 1) * size] = product[start : start + size]
            reduce_copy(q, 0).start()

    def finish_c():
        grad_c = r.gc[...] + mm_tn(r.gscores[...].astype(BF16), r.proj[:, :state_dim])
        grad_c = grad_c.astype(BF16)
        r.gproj[:, state_dim : 2 * state_dim] = grad_c
        plane_start(1, mm(r.layer_t[...], grad_c))

    def finish_b():
        grad_b = r.gb[...] + mm(r.gscores[...].astype(BF16), r.proj[:, state_dim:])
        grad_b = grad_b.astype(BF16)
        r.gproj[:, :state_dim] = grad_b
        plane_start(0, mm(r.layer_t[...], grad_b))

    def finish_dt():
        raw, step, run = r.raw[...], r.step[...], r.run[...]
        rate = jnp.exp(rate_ref[...])
        total = run[tokens - 1 :, :]
        upper = triangle(tokens, lambda a, b: a <= b)
        lower = triangle(tokens, lambda a, b: a > b)
        inner = r.rows[:, 0, :].T + r.reads[...] - r.cols[...]
        grad_decay = (
            exact_mm(upper, inner) + exact_mm(lower, step * r.backs[...])
            + jnp.exp(total) * r.cross[0:1]
        )
        sigmoid = 1.0 / (1.0 + jnp.exp(-raw))
        grad_raw = (r.gsteps[...] - rate * grad_decay) * sigmoid
        narrow = grad_raw.astype(BF16)
        r.gproj[:, 2 * state_dim :] = narrow
        shift_row = lax.broadcasted_iota(jnp.int32, (heads, lanes * TILE), 0)
        shift_col = lax.broadcasted_iota(jnp.int32, (heads, lanes * TILE), 1)
        shift = jnp.zeros(shift_row.shape, F32)
        for j in range(lanes):
            shift = jnp.where(shift_col == shift_row + j * (TILE + heads), 1.0, shift)
        moved = mm(narrow, shift.astype(BF16)).astype(BF16)
        product = mm(r.layer_t[...], moved)
        q = len(plan) - 1
        unit = group + 8
        sums = getattr(r, f"sum{q}")
        where = places(plan[q][3])
        small = jnp.concatenate([
            jnp.sum(grad_raw, axis=0, keepdims=True),
            -rate * jnp.sum(grad_decay * step, axis=0, keepdims=True),
            r.skips[0:1],
            jnp.zeros((5, heads), F32),
        ], axis=0)
        small = jnp.concatenate([small, jnp.zeros((8, TILE - heads), F32)], axis=1)
        for shard in range(devices):
            start = where[shard] * unit
            packed = jnp.zeros((group, TILE), F32)
            for j in range(lanes):
                count = min(share - j * group, group)
                if count <= 0:
                    continue
                first = shard * share + j * group
                piece = product[first : first + count, j * TILE : (j + 1) * TILE]
                if count < group:
                    piece = jnp.concatenate(
                        [piece, jnp.zeros((group - count, TILE), F32)], axis=0)
                packed = packed + piece
            sums[start : start + group] = packed
            sums[start + group : start + unit] = small
        reduce_copy(q, 0).start()

    def layer_tail():
        r.glayer[...] = (
            mm_nt(r.gproj[:, : 2 * state_dim], r.wbc[...])
            + mm(r.gproj[:, 2 * state_dim :], r.wdt[...])
        ).astype(BF16)
        stores[1].start()

    stores = [
        pltpu.make_async_copy(r.gvalues, gvalues_hbm, r.store.at[0]),
        pltpu.make_async_copy(r.glayer, glayer_hbm, r.store.at[1]),
    ]

    def prepare():
        run = r.run[...]
        run_rows = run.T
        for head in range(heads):
            r.run_rows[head] = run_rows[head : head + 1]
        for i, piece in enumerate(three_way(run)):
            r.parts[i] = piece
        r.scores[...] = mm_nt(r.proj[:, :state_dim], r.proj[:, state_dim:])
        r.gscores[...] = jnp.zeros_like(r.gscores)

    def turn():
        r.layer_t[...] = r.layer[...].T

    def body(pair, _):
        inner_pair(pair, heads, r.u, r.grad, r.scores, r.parts, r.run_rows,
                   r.gu, r.rows, r.gscores, head_size)
        return 0

    events = []

    def event(time, work, *args):
        events.append((time, len(events), functools.partial(work, *args)))

    n = CHUNKS
    make, wire, flight, near, hop = 0.5, 1.5, 2.3, 1.4, 3.7
    base = make + near
    for k in range(n):
        event(make * k, make_states, "s", k)
        event(make * (k + 1) + near, pair_up, "s", k)
        event(make * (n + k), make_states, "g", k)
        event(make * (n + k + 1) + near, pair_up, "g", k)
        for i, kind in enumerate(kinds):
            arrive = base + wire * (i * n + k + 1) + flight
            event(arrive, row_up, kind, k)
            for place in range(zrows):
                event(arrive + hop * min(place, 3) + 0.01, chain_slot, kind, k, place)
            back = base + wire * ((2 + i) * n + k + 1) + flight
            event(back + 0.1, chip_down, kind, k)
            event(back + near, forward_tail if kind == "s" else backward_tail, k)
    event(make * 2 * n + 0.05, prepare)
    event(make * 2 * n + 8.0, turn)
    c_time = base + wire * 3 * n + flight + near + 0.2
    inner_time = base + wire * 2 * n + flight
    for k in range(n):
        event(inner_time + 0.02 * k, inner_tail, k)
    event(c_time, finish_c)
    b_time = base + wire * 4 * n + flight + near + 0.2
    event(b_time, finish_b)
    event(b_time + 0.1, stores[0].start)
    event(b_time + 0.2, finish_dt)
    event(b_time + 0.3, layer_tail)
    for q, (plane, first, size, order) in enumerate(plan):
        time = (c_time if plane == 1 else b_time + 1.0) + 0.2
        if plane == 2:
            time = time + 0.4
        piece = 1 if first > 0 else 0
        pace = 3.6 * size / 80
        for i in range(levels):
            if i == 0:
                time = time + 1.4 + 0.5 * piece
            else:
                time = time + pace * (1 + piece * (i == 1)) + 2.3
                pace = pace / 2
            event(time, reduce_step, q, i)
    events.sort(key=lambda item: item[:2])

    pairs = width // TILE
    pair_time = 0.42
    done, clock, begun = 0, 0.0, False
    for time, index, work in events:
        if begun and done < pairs:
            take = min(pairs - done, int((time - clock) / pair_time))
            if time >= inner_time:
                take = pairs - done
            if take >= 2 or (take > 0 and done + take == pairs):
                lax.fori_loop(done, done + take, body, 0)
                done += take
                clock = clock + take * pair_time
        work()
        clock = max(clock, time)
        if work.func is prepare:
            begun = True
            clock = time + 0.3

    for q, (plane, first, size, order) in enumerate(plan):
        unit = size
        start = pl.multiple_of(offset(order, levels) * unit, 8)
        result = getattr(r, f"sum{q}")[pl.ds(start, unit)]
        if plane < 2:
            gbc_ref[first : first + size, plane * TILE : (plane + 1) * TILE] = result
        else:
            last_ref[...] = result
    for store in stores:
        store.wait()
    for k in range(2):
        tot_copy(k).wait_send()
    for kind in kinds:
        for k in range(n):
            for stage in (0, 1, 3, 4):
                copy(stage, kind, k).wait_send()
        if zrows > 1:
            sends = row < zrows - 1 if kind == "s" else row > 0

            @pl.when(sends)
            def _(kind=kind):
                for k in range(n):
                    copy(2, kind, k).wait_send()
    for q in range(len(plan)):
        for i in range(levels):
            reduce_copy(q, i).wait_send()


def finish_kernel(heads, group, lanes, gvalues_in, glayer_in, gbc_in, last_in,
                  gvalues_ref, glayer_ref, gbc_ref, gdt_ref, gbias_ref, grate_ref, gskip_ref):
    gvalues_ref[...] = gvalues_in[...]
    glayer_ref[...] = glayer_in[...]
    gbc_ref[...] = gbc_in[...]
    last = last_in[...]
    share = gdt_ref.shape[0]
    for j in range(lanes):
        count = min(share - j * group, group)
        if count > 0:
            gdt_ref[j * group : j * group + count] = last[:count, j * heads : (j + 1) * heads]
    gbias_ref[...] = last[group : group + 1, :heads]
    grate_ref[...] = last[group + 1 : group + 2, :heads]
    gskip_ref[...] = last[group + 2 : group + 3, :heads]


def local(layer_in, ssm_in, weight_bc, weight_dt, bias_dt, log_rate, skip_gain, grad_out):
    tokens, depth = layer_in.shape
    heads = log_rate.shape[0]
    width = ssm_in.shape[1]
    state_dim = weight_bc.shape[1] // 2
    devices = lax.axis_size("seq")
    share, lanes, group = packing(depth, devices, heads)
    scratch = scratch_list(tokens, depth, width, heads, state_dim, devices)
    shape = jax.ShapeDtypeStruct
    gvalues, glayer, gbc, last = pl.pallas_call(
        functools.partial(mega_kernel, devices, list(scratch)),
        out_shape=[
            shape((tokens, width), BF16),
            shape((tokens, depth), BF16),
            shape((share, 2 * state_dim), F32),
            shape((group + 8, TILE), F32),
        ],
        in_specs=[ANY] * 4 + [VMEM] * 3 + [ANY],
        out_specs=[ANY, ANY, VMEM, VMEM],
        scratch_shapes=list(scratch.values()),
        compiler_params=pltpu.CompilerParams(
            collective_id=0, has_side_effects=True, vmem_limit_bytes=VMEM_LIMIT
        ),
        name="mixer",
    )(layer_in, ssm_in, weight_bc, weight_dt.T, bias_dt[None, :], log_rate[None, :],
      skip_gain[None, :], grad_out)
    outs = pl.pallas_call(
        functools.partial(finish_kernel, heads, group, lanes),
        out_shape=[
            shape((tokens, width), BF16),
            shape((tokens, depth), BF16),
            shape((share, 2 * state_dim), F32),
            shape((share, heads), F32),
            shape((1, heads), F32),
            shape((1, heads), F32),
            shape((1, heads), F32),
        ],
        in_specs=[VMEM] * 4,
        out_specs=[VMEM] * 7,
        compiler_params=pltpu.CompilerParams(vmem_limit_bytes=VMEM_LIMIT),
        name="finish",
    )(gvalues, glayer, gbc, last)
    return tuple(outs[:4]) + tuple(out[0] for out in outs[4:])


def solution(mesh):
    rows = P(("groups", "seq"), None)
    in_specs = (rows, rows, P(), P(), P(), P(), P(), rows)
    out_specs = (rows, rows, rows, rows, P("groups"), P("groups"), P("groups"))
    return jax.shard_map(local, mesh=mesh, in_specs=in_specs, out_specs=out_specs, check_vma=False)
```

time: 128 us -> 93.1 us (0.73)
  Pallas kernels: 121 us -> 90.7 us
  local copies, waits for them, and re-layouts: 6.66 us -> 1.58 us
    pallas_call x4 -> x2, Pallas kernels: 121 us -> 90.7 us  [the longest x1 87.3 us: local(): pl.pallas_call(functools.partial(mega_kernel, devices, list(scratch)), ou...]
    unnamed x5 -> x1, local copies, waits for them, and re-layouts: 6.66 us -> 1.58 us
where the time goes in v1:
time: 93.1 us; the launch traced here: 92.9 us
  Pallas kernels  90.7 us (97%)
  local copies, waits for them, and re-layouts  1.58 us (2%)
    pallas_call x1, Pallas kernels, local(): pl.pallas_call(functools.partial(mega_kernel, devices, list(scratch)), ou...  87.3 us
    pallas_call x1, Pallas kernels, local(): pl.pallas_call(functools.partial(finish_kernel, heads, group, lanes), out...  3.38 us

profile of v1, /device:TPU:0, one launch (start us, length us, event | category | flops | bytes accessed | tf_op | source)
XLA Modules:
  0.0 92.9 jit_solution(17017074136004857662)
XLA Ops:
  0.6 87.3 %mixer.1 = (bf16[256,2560]{1,0:T(8,128)(2,1)}, bf16[256,2560]{1,0:T(8,128)(2,1)}, f32[160,256]{1,0:T(8,128)}, f32[64,128]{1,0:T(8,128)}) custom-call(bf16[256,2560]{1,0:T(8,128)(2,1)} %layer_hbm.1, bf16[256,2560]{1,0:T(8,128)(2,1)} %values_hbm.1, bf16[2560,256]{1,0:T(8,128)(2,1)} %wbc_hbm.1, bf16[40,2560]{1,0:T(8,128)(2,1)} %bitcast.7, f32[1,40]{1,0:T(1,128)} %bitcast.8, ...), custom_call_target="tpu_custom_call" | custom-call | tf_op jit(solution)/shard_map/mixer/pallas_call | solution.py:718
  88.0 3.4 %finish.1 = (bf16[256,2560]{1,0:T(8,128)(2,1)}, bf16[256,2560]{1,0:T(8,128)(2,1)}, f32[160,256]{1,0:T(8,128)}, f32[160,40]{1,0:T(8,128)}, f32[1,40]{1,0:T(1,128)}, /*index=5*/f32[1,40]{1,0:T(1,128)}, f32[1,40]{1,0:T(1,128)}) custom-call(bf16[256,2560]{1,0:T(8,128)(2,1)} %get-tuple-element.18.gvalues_in, bf16[256,2560]{1,0:T(8,128)(2,1)} %get-tuple-element.19.glayer_in, ...), custom_call_target="tpu_custom_call" | custom-call | tf_op jit(solution)/shard_map/finish/pallas_call | solution.py:735
  91.3 1.6 %copy.15 = f32[160,40]{0,1:T(8,128)} copy(f32[160,40]{1,0:T(8,128)} %get-tuple-element.32) | data formatting | bytes 51200

commit v2 on v1

--- a/solution.py
+++ b/solution.py
@@ -9,8 +9,10 @@
 F32 = jnp.float32
 BF16 = jnp.bfloat16
 TILE = 128
-CHUNKS = 5
-VMEM_LIMIT = 60 * 1024 * 1024
+CHUNKS = 10
+BLOCK = 2
+REDUCE_C, REDUCE_B, REDUCE_DT = "zzyy", "yyyy", "z"
+VMEM_LIMIT = 52 * 1024 * 1024
 VMEM = pl.BlockSpec(memory_space=pltpu.VMEM)
 ANY = pl.BlockSpec(memory_space=pl.ANY)
 
@@ -41,8 +43,23 @@
     return jnp.where(inside, 1.0, 0.0).astype(BF16)
 
 
-def spread(parts, hot):
-    return mm(parts[0], hot) + mm(parts[1], hot) + mm(parts[2], hot)
+def one_hot_stacked(heads, width, columns, first=0):
+    row = lax.rem(lax.broadcasted_iota(jnp.int32, (TILE, columns), 0), heads)
+    real = lax.broadcasted_iota(jnp.int32, (TILE, columns), 0) < 3 * heads
+    col = lax.broadcasted_iota(jnp.int32, (TILE, columns), 1) + first
+    inside = (col >= row * width) & (col < (row + 1) * width) & real
+    return jnp.where(inside, 1.0, 0.0).astype(BF16)
+
+
+def stacked(x):
+    rows, heads = x.shape
+    zero = jnp.zeros((rows, TILE - heads), F32)
+    result = None
+    for i, piece in enumerate(three_way(x)):
+        piece = jnp.concatenate([piece.astype(F32), zero], axis=1)
+        piece = piece if i == 0 else pltpu.roll(piece, i * heads, 1)
+        result = piece if i == 0 else result + piece
+    return result.astype(BF16)
 
 
 def head_sum(x, hot):
@@ -70,8 +87,8 @@
     cols = pl.ds(pl.multiple_of(pair * TILE, TILE), TILE)
     lane = lax.broadcasted_iota(jnp.int32, (TILE, TILE), 1)
     causal = lax.broadcasted_iota(jnp.int32, (TILE, TILE), 0) <= lane
-    wide = one_hot(heads, TILE, per * TILE, pair * (per * TILE))
-    run_cols = spread([parts_ref[i] for i in range(3)], wide)
+    wide = one_hot_stacked(heads, TILE, per * TILE, pair * (per * TILE))
+    run_cols = mm(parts_ref[...], wide)
     grads = [grad_ref[t * TILE : (t + 1) * TILE, cols] for t in range(blocks)]
     gus = [jnp.zeros((TILE, TILE), F32) for _ in range(blocks)]
     for sub in range(per):
@@ -108,18 +125,26 @@
     return share, lanes, group
 
 
+def pieces_of(share):
+    units = share // 16
+    if share % 16 or units < 4:
+        return [share]
+    return [16 * ((units + 3 - i) // 4) for i in range(4)]
+
+
 def reduce_plan(depth, devices, heads):
     share, lanes, group = packing(depth, devices, heads)
     levels = devices.bit_length() - 1
     y_first = list(range(levels))
     z_first = [0] + list(range(2, levels)) + [1]
-    pieces = 2 if share % 32 == 0 else 1
-    plan = []
-    for plane, order in ((1, z_first), (0, y_first)):
-        for piece in range(pieces):
-            size = share // pieces
-            plan.append((plane, piece * size, size, order))
-    plan.append((2, 0, group + 8, y_first))
+    plan, first = [], 0
+    cuts = pieces_of(share)
+    for plane, names in ((1, REDUCE_C), (0, REDUCE_B)):
+        first = 0
+        for piece, size in enumerate(cuts):
+            plan.append((plane, first, size, y_first if names[piece] == "y" else z_first))
+            first += size
+    plan.append((2, 0, group + 8, y_first if REDUCE_DT == "y" else z_first))
     return plan
 
 
@@ -141,7 +166,13 @@
     add("proj", (tokens, 2 * state_dim), BF16)
     add("proj_t", (2 * state_dim, tokens), BF16)
     add("hot", (TILE, width), BF16)
-    add("parts", (3, tokens, heads), BF16)
+    for name in ("parts", "step3", "tail3", "lead3"):
+        add(name, (tokens, TILE), BF16)
+    add("hot3", (TILE, width), BF16)
+    for name in ("bias", "rate", "gain"):
+        add(name, (1, heads))
+    add("pre", (tokens, heads))
+    add("sigmoid", (tokens, heads))
     for name in ("raw", "step", "run"):
         add(name, (tokens, heads))
     add("run_rows", (heads, 1, tokens))
@@ -156,11 +187,10 @@
         add(name, (tokens, heads))
     add("cross", (8, heads))
     add("skips", (8, heads))
+    add("small", (8, TILE))
     add("gc", (tokens, state_dim))
     add("gb", (tokens, state_dim))
     add("gproj", (tokens, 2 * state_dim + heads), BF16)
-    add("gvalues", (tokens, width), BF16)
-    add("glayer", (tokens, depth), BF16)
     for kind in ("s", "g"):
         add("st_" + kind, (state_dim, width))
         add("get0_" + kind, (half, width))
@@ -181,8 +211,7 @@
         for i in range(levels):
             add(f"rget{q}_{i}", ((devices >> (i + 1)) * size, TILE))
     add_sem = lambda name, shape: names.__setitem__(name, pltpu.SemaphoreType.DMA(shape))
-    add_sem("load", (5,))
-    add_sem("store", (2,))
+    add_sem("load", (8,))
     add_sem("comm", (2, 5, 2, CHUNKS))
     add_sem("tot_sems", (2, 2))
     add_sem("rsem", (2, levels, len(plan)))
@@ -193,14 +222,14 @@
     pass
 
 
-def mega_kernel(devices, names, layer_hbm, values_hbm, wbc_hbm, wdt_hbm, bias_ref, rate_ref,
-                gain_ref, grad_hbm, gvalues_hbm, glayer_hbm, gbc_ref, last_ref, *refs):
+def mega_kernel(devices, names, layer_hbm, values_hbm, wbc_hbm, wdt_hbm, bias_hbm, rate_hbm,
+                gain_hbm, grad_hbm, gvalues_ref, glayer_ref, gbc_ref, last_ref, *refs):
     r = Box()
     for name, ref in zip(names, refs):
         setattr(r, name, ref)
     tokens, depth = r.layer.shape
     width = r.values.shape[1]
-    heads = bias_ref.shape[1]
+    heads = r.bias.shape[1]
     head_size = width // heads
     state_dim = r.st_s.shape[0]
     half, quarter = state_dim // 2, state_dim // 4
@@ -220,10 +249,11 @@
         for i, (source, target) in enumerate((
             (layer_hbm, r.layer), (wbc_hbm, r.wbc), (wdt_hbm, r.wdt),
             (values_hbm, r.values), (grad_hbm, r.grad),
+            (bias_hbm, r.bias), (rate_hbm, r.rate), (gain_hbm, r.gain),
         ))
     ]
-    for load in loads:
-        load.start()
+    for i in (0, 1, 2, 5, 6, 7, 3, 4):
+        loads[i].start()
 
     barrier = pltpu.get_barrier_semaphore()
     for k in range(levels):
@@ -238,21 +268,25 @@
             pl.semaphore_signal(barrier, inc=1, device_id={"seq": down_row}, device_id_type=mesh_id)
 
     r.hot[...] = one_hot(TILE, head_size, width)
+    r.hot3[...] = one_hot_stacked(heads, head_size, width)
     loads[0].wait()
     loads[1].wait()
     layer = r.layer[...]
     proj = mm(layer, r.wbc[...]).astype(BF16)
     r.proj[...] = proj
     r.proj_t[...] = proj.T
-    loads[2].wait()
-    raw = mm_nt(layer, r.wdt[...]) + bias_ref[...]
+    for i in (2, 5, 6, 7):
+        loads[i].wait()
+    raw = mm_nt(layer, r.wdt[...]) + r.bias[...]
     r.raw[...] = raw
     step = jnp.maximum(raw, 0.0) + jnp.log1p(jnp.exp(-jnp.abs(raw)))
     r.step[...] = step
-    decay = -jnp.exp(rate_ref[...]) * step
+    decay = -jnp.exp(r.rate[...]) * step
     run = exact_mm(triangle(tokens, lambda a, b: a >= b), decay)
     r.run[...] = run
     total = run[tokens - 1 :, :]
+    r.step3[...] = stacked(step)
+    r.tail3[...] = stacked(jnp.exp(total - run))
     r.tots[0] = jnp.zeros((8, TILE), F32)
     r.tots[0, :, :heads] = jnp.broadcast_to(total, (8, heads))
     if zrows > 1:
@@ -321,16 +355,15 @@
 
     first0, first1 = bits[0] == 0, bits[1] == 0
 
-    def make_states(kind, k):
-        if k == 0:
+    def make_states(kind, block):
+        if block == 0:
             loads[3 if kind == "s" else 4].wait()
-        cols = cols_of(k)
-        hot = r.hot[:heads, cols]
+        cols = slice(block * BLOCK * span, (block + 1) * BLOCK * span)
+        hot = r.hot3[:, cols]
         if kind == "s":
-            step_w = spread(three_way(r.step[...]), hot)
+            step_w = mm(r.step3[...], hot)
             r.step_w[:, cols] = step_w
-            run = r.run[...]
-            tail_w = spread(three_way(jnp.exp(run[tokens - 1 :, :] - run)), hot)
+            tail_w = mm(r.tail3[...], hot)
             r.tail_w[:, cols] = tail_w
             u = step_w * r.values[:, cols].astype(F32)
             r.u[:, cols] = u.astype(BF16)
@@ -338,12 +371,15 @@
             r.tsv[:, cols] = tsv
             r.st_s[:, cols] = mm(r.proj_t[:state_dim], tsv)
         else:
-            lead_w = spread(three_way(jnp.exp(r.run[...])), hot)
+            if block == 0:
+                r.lead3[...] = stacked(jnp.exp(r.run[...]))
+            lead_w = mm(r.lead3[...], hot)
             r.lead_w[:, cols] = lead_w
             lg = (lead_w * r.grad[:, cols].astype(F32)).astype(BF16)
             r.lg[:, cols] = lg
             r.st_g[:, cols] = mm(r.proj_t[state_dim:], lg)
-        copy(0, kind, k).start()
+        for k in range(block * BLOCK, (block + 1) * BLOCK):
+            copy(0, kind, k).start()
 
     def merge(kind, first, mine, got, e_mine, e_other):
         if kind == "s":
@@ -357,8 +393,6 @@
         return jnp.where(first, far, parent), jnp.where(first, parent, near)
 
     def pair_up(kind, k):
-        if kind == "s" and k == 0:
-            tot_done(0)
         copy(0, kind, k).wait_recv()
         cols = cols_of(k)
         mine = at("st", kind)[rows_at(bits[0], half), cols]
@@ -368,8 +402,6 @@
         copy(1, kind, k).start()
 
     def row_up(kind, k):
-        if kind == "s" and k == 0:
-            tot_done(1)
         copy(1, kind, k).wait_recv()
         cols = cols_of(k)
         mine = at("agg1", kind)[rows_at(bits[1], quarter), cols]
@@ -390,6 +422,12 @@
                 passed = r.decays[4, 0:1, cols] * parent + passed
             at("zout", kind)[:, cols] = passed
             copy(2, kind, k).start()
+        if place == 0:
+            at("zin", kind)[:, cols] = parent
+
+    def row_down(kind, k):
+        cols = cols_of(k)
+        parent = at("zin", kind)[:, cols]
         mine = at("agg1", kind)[rows_at(bits[1], quarter), cols]
         got = at("get1", kind)[:, cols]
         kept, sent = split(kind, first1, parent, mine, got,
@@ -452,8 +490,8 @@
         gather("gsteps", k, head_sum(values * gu, hot))
         cross = jnp.sum(r.end_s[:, cols] * outgoing, axis=0, keepdims=True)
         gather("cross", k, head_sum(jnp.broadcast_to(cross, (8, span)), hot))
-        gain = spread(three_way(jnp.broadcast_to(gain_ref[...], (8, heads))), hot)[0:1]
-        r.gvalues[:, cols] = (
+        gain = mm(stacked(jnp.broadcast_to(r.gain[...], (8, heads))), r.hot3[:, cols])[0:1]
+        gvalues_ref[:, cols] = (
             r.step_w[:, cols] * gu + gain * r.grad[:, cols].astype(F32)
         ).astype(BF16)
 
@@ -493,62 +531,71 @@
         if i + 1 < levels:
             reduce_copy(q, i + 1).start()
 
-    def plane_start(plane, product):
-        for q, (owner, first, size, order) in enumerate(plan):
-            if owner != plane:
-                continue
-            sums = getattr(r, f"sum{q}")
-            where = places(order)
-            for shard in range(devices):
-                start = shard * share + first
-                sums[where[shard] * size : (where[shard] + 1) * size] = product[start : start + size]
-            reduce_copy(q, 0).start()
+    def send_piece(q):
+        plane, first, size, order = plan[q]
+        grad = r.gproj[:, plane * state_dim : (plane + 1) * state_dim]
+        sums = getattr(r, f"sum{q}")
+        where = places(order)
+        product = mm(r.layer_t[devices * first : devices * (first + size)], grad)
+        for shard in range(devices):
+            sums[where[shard] * size : (where[shard] + 1) * size] = (
+                product[shard * size : (shard + 1) * size])
+        reduce_copy(q, 0).start()
 
     def finish_c():
         grad_c = r.gc[...] + mm_tn(r.gscores[...].astype(BF16), r.proj[:, :state_dim])
         grad_c = grad_c.astype(BF16)
         r.gproj[:, state_dim : 2 * state_dim] = grad_c
-        plane_start(1, mm(r.layer_t[...], grad_c))
 
     def finish_b():
         grad_b = r.gb[...] + mm(r.gscores[...].astype(BF16), r.proj[:, state_dim:])
         grad_b = grad_b.astype(BF16)
         r.gproj[:, :state_dim] = grad_b
-        plane_start(0, mm(r.layer_t[...], grad_b))
+
+    def before_dt():
+        upper = triangle(tokens, lambda a, b: a <= b)
+        inner = r.rows[:, 0, :].T + r.reads[...] - r.cols[...]
+        r.pre[...] = exact_mm(upper, inner)
+        r.sigmoid[...] = 1.0 / (1.0 + jnp.exp(-r.raw[...]))
 
     def finish_dt():
-        raw, step, run = r.raw[...], r.step[...], r.run[...]
-        rate = jnp.exp(rate_ref[...])
-        total = run[tokens - 1 :, :]
-        upper = triangle(tokens, lambda a, b: a <= b)
+        step = r.step[...]
+        rate = jnp.exp(r.rate[...])
+        total = r.run[tokens - 1 :, :]
         lower = triangle(tokens, lambda a, b: a > b)
-        inner = r.rows[:, 0, :].T + r.reads[...] - r.cols[...]
         grad_decay = (
-            exact_mm(upper, inner) + exact_mm(lower, step * r.backs[...])
-            + jnp.exp(total) * r.cross[0:1]
+            r.pre[...] + exact_mm(lower, step * r.backs[...]) + jnp.exp(total) * r.cross[0:1]
         )
-        sigmoid = 1.0 / (1.0 + jnp.exp(-raw))
-        grad_raw = (r.gsteps[...] - rate * grad_decay) * sigmoid
-        narrow = grad_raw.astype(BF16)
-        r.gproj[:, 2 * state_dim :] = narrow
-        shift_row = lax.broadcasted_iota(jnp.int32, (heads, lanes * TILE), 0)
-        shift_col = lax.broadcasted_iota(jnp.int32, (heads, lanes * TILE), 1)
-        shift = jnp.zeros(shift_row.shape, F32)
-        for j in range(lanes):
-            shift = jnp.where(shift_col == shift_row + j * (TILE + heads), 1.0, shift)
-        moved = mm(narrow, shift.astype(BF16)).astype(BF16)
-        product = mm(r.layer_t[...], moved)
-        q = len(plan) - 1
-        unit = group + 8
-        sums = getattr(r, f"sum{q}")
-        where = places(plan[q][3])
+        grad_raw = (r.gsteps[...] - rate * grad_decay) * r.sigmoid[...]
+        r.gproj[:, 2 * state_dim :] = grad_raw.astype(BF16)
         small = jnp.concatenate([
             jnp.sum(grad_raw, axis=0, keepdims=True),
             -rate * jnp.sum(grad_decay * step, axis=0, keepdims=True),
             r.skips[0:1],
             jnp.zeros((5, heads), F32),
         ], axis=0)
-        small = jnp.concatenate([small, jnp.zeros((8, TILE - heads), F32)], axis=1)
+        r.small[...] = jnp.concatenate([small, jnp.zeros((8, TILE - heads), F32)], axis=1)
+
+    def send_dt():
+        narrow = r.gproj[:, 2 * state_dim :]
+        product = mm(r.layer_t[...], jnp.concatenate(
+            [narrow.astype(F32), jnp.zeros((tokens, TILE - heads), F32)], axis=1).astype(BF16))
+        small = r.small[...]
+
+        def shard_rows(shard, begin, count):
+            found, first = [], 0
+            for size in pieces_of(share):
+                low, high = max(begin, first), min(begin + count, first + size)
+                if low < high:
+                    base = devices * first + shard * size - first
+                    found.append(product[base + low : base + high])
+                first += size
+            return found[0] if len(found) == 1 else jnp.concatenate(found, axis=0)
+
+        q = len(plan) - 1
+        unit = group + 8
+        sums = getattr(r, f"sum{q}")
+        where = places(plan[q][3])
         for shard in range(devices):
             start = where[shard] * unit
             packed = jnp.zeros((group, TILE), F32)
@@ -556,8 +603,9 @@
                 count = min(share - j * group, group)
                 if count <= 0:
                     continue
-                first = shard * share + j * group
-                piece = product[first : first + count, j * TILE : (j + 1) * TILE]
+                piece = shard_rows(shard, j * group, count)
+                if j > 0:
+                    piece = pltpu.roll(piece, j * heads, 1)
                 if count < group:
                     piece = jnp.concatenate(
                         [piece, jnp.zeros((group - count, TILE), F32)], axis=0)
@@ -567,29 +615,28 @@
         reduce_copy(q, 0).start()
 
     def layer_tail():
-        r.glayer[...] = (
+        glayer_ref[...] = (
             mm_nt(r.gproj[:, : 2 * state_dim], r.wbc[...])
             + mm(r.gproj[:, 2 * state_dim :], r.wdt[...])
         ).astype(BF16)
-        stores[1].start()
-
-    stores = [
-        pltpu.make_async_copy(r.gvalues, gvalues_hbm, r.store.at[0]),
-        pltpu.make_async_copy(r.glayer, glayer_hbm, r.store.at[1]),
-    ]
 
     def prepare():
         run = r.run[...]
         run_rows = run.T
         for head in range(heads):
             r.run_rows[head] = run_rows[head : head + 1]
-        for i, piece in enumerate(three_way(run)):
-            r.parts[i] = piece
+        r.parts[...] = stacked(run)
         r.scores[...] = mm_nt(r.proj[:, :state_dim], r.proj[:, state_dim:])
         r.gscores[...] = jnp.zeros_like(r.gscores)
 
     def turn():
-        r.layer_t[...] = r.layer[...].T
+        turned = r.layer[...].T
+        first = 0
+        for size in pieces_of(share):
+            for shard in range(devices):
+                start, target = shard * share + first, devices * first + shard * size
+                r.layer_t[target : target + size] = turned[start : start + size]
+            first += size
 
     def body(pair, _):
         inner_pair(pair, heads, r.u, r.grad, r.scores, r.parts, r.run_rows,
@@ -598,69 +645,118 @@
 
     events = []
 
-    def event(time, work, *args):
-        events.append((time, len(events), functools.partial(work, *args)))
+    def event(time, cost, work, *args):
+        events.append((time, len(events), cost, functools.partial(work, *args)))
 
     n = CHUNKS
-    make, wire, flight, near, hop = 0.5, 1.5, 2.3, 1.4, 3.7
-    base = make + near
+    wire, flight, near, hop = 7.05 / n, 3.0, 1.05, 2.9 + 7.2 / n
+    start, blocks = 3.9, n // BLOCK
+    make_s, make_g = 2.25 / blocks, 1.95 / blocks
+    first = start + make_s + near
+    event(start + 2 * make_s - 0.01, 0.27, tot_done, 0)
+    event(first + 2.2, 0.25, tot_done, 1)
+    for block in range(blocks):
+        event(start + make_s * block, make_s, make_states, "s", block)
+        event(start + make_s * blocks + make_g * block, make_g, make_states, "g", block)
     for k in range(n):
-        event(make * k, make_states, "s", k)
-        event(make * (k + 1) + near, pair_up, "s", k)
-        event(make * (n + k), make_states, "g", k)
-        event(make * (n + k + 1) + near, pair_up, "g", k)
+        block = k // BLOCK
+        event(start + make_s * (block + 1) + near, 0.02, pair_up, "s", k)
+        event(start + make_s * blocks + make_g * (block + 1) + near + 0.3, 0.02, pair_up, "g", k)
         for i, kind in enumerate(kinds):
-            arrive = base + wire * (i * n + k + 1) + flight
-            event(arrive, row_up, kind, k)
+            arrive = first + wire * (i * n + k + 1) + flight
+            event(arrive, 0.02, row_up, kind, k)
             for place in range(zrows):
-                event(arrive + hop * min(place, 3) + 0.01, chain_slot, kind, k, place)
-            back = base + wire * ((2 + i) * n + k + 1) + flight
-            event(back + 0.1, chip_down, kind, k)
-            event(back + near, forward_tail if kind == "s" else backward_tail, k)
-    event(make * 2 * n + 0.05, prepare)
-    event(make * 2 * n + 8.0, turn)
-    c_time = base + wire * 3 * n + flight + near + 0.2
-    inner_time = base + wire * 2 * n + flight
-    for k in range(n):
-        event(inner_time + 0.02 * k, inner_tail, k)
-    event(c_time, finish_c)
-    b_time = base + wire * 4 * n + flight + near + 0.2
-    event(b_time, finish_b)
-    event(b_time + 0.1, stores[0].start)
-    event(b_time + 0.2, finish_dt)
-    event(b_time + 0.3, layer_tail)
-    for q, (plane, first, size, order) in enumerate(plan):
-        time = (c_time if plane == 1 else b_time + 1.0) + 0.2
-        if plane == 2:
-            time = time + 0.4
-        piece = 1 if first > 0 else 0
-        pace = 3.6 * size / 80
-        for i in range(levels):
-            if i == 0:
-                time = time + 1.4 + 0.5 * piece
+                event(arrive + hop * min(place, 3) + 0.01, 0.02, chain_slot, kind, k, place)
+            down = max(first + wire * (2 + i) * n, first + wire * (i * n + 1) + flight + 3 * hop)
+            down = down + wire * k
+            event(max(arrive + 3 * hop, down - 1.0) + 0.02, 0.02, row_down, kind, k)
+            event(down + wire + flight, 0.02, chip_down, kind, k)
+            arrive = down + wire + flight + near
+            if kind == "s":
+                event(arrive + 0.4, 3.4 / n, forward_tail, k)
             else:
-                time = time + pace * (1 + piece * (i == 1)) + 2.3
-                pace = pace / 2
-            event(time, reduce_step, q, i)
+                event(arrive + 0.2, 5.0 / n, backward_tail, k)
+            if k == n - 1 and kind == "s":
+                c_time = arrive + 0.5
+                event(c_time, 0.2, finish_c)
+            elif k == n - 1:
+                b_time = arrive + 0.3
+                event(b_time, 0.2, finish_b)
+                event(b_time + 1.5, 0.4, finish_dt)
+                event(b_time + 2.0, 0.8, send_dt)
+                event(b_time + 5.0, 1.4, layer_tail)
+    free = {"z": 0.0, "m": 0.0, "y": first + 4 * n * wire}
+    clocks = []
+    for q, (plane, offset_rows, size, order) in enumerate(plan):
+        piece = q % len(pieces_of(share))
+        if plane == 1:
+            made = c_time + 0.2 + 0.5 * piece
+        elif plane == 0:
+            made = b_time + 0.2 + 0.3 * piece
+        else:
+            made = b_time + 2.5
+        if plane < 2:
+            event(made, 0.3, send_piece, q)
+        ready = made + 0.3 + 1.1
+        if plane == 1 and order[1] == 1:
+            ready = max(ready, down + 0.1)
+        clocks.append([ready, size * 0.045])
+        event(clocks[q][0], 0.04, reduce_step, q, 0)
+    pending = [(clocks[q][0], q, 1) for q in range(len(plan))]
+    while pending:
+        pending.sort()
+        ready, q, i = pending.pop(0)
+        level = plan[q][3][i]
+        pace = clocks[q][1]
+        clocks[q][1] = pace / 2
+        begin = max(ready, free["y" if level == 1 else "z"])
+        if level == 1:
+            free["y"] = begin + pace
+            done_at = begin + pace + 2.8
+        elif level == 2:
+            free["z"] = begin + pace
+            done_at = begin + pace + 2.8
+        else:
+            free["z"] = begin + pace
+            free["m"] = max(begin, free["m"]) + 2 * pace
+            done_at = free["m"] + 3.5
+        event(done_at, 0.03, reduce_step, q, i)
+        if i + 1 < levels:
+            pending.append((done_at, q, i + 1))
     events.sort(key=lambda item: item[:2])
 
     pairs = width // TILE
-    pair_time = 0.42
-    done, clock, begun = 0, 0.0, False
-    for time, index, work in events:
-        if begun and done < pairs:
-            take = min(pairs - done, int((time - clock) / pair_time))
-            if time >= inner_time:
-                take = pairs - done
-            if take >= 2 or (take > 0 and done + take == pairs):
-                lax.fori_loop(done, done + take, body, 0)
-                done += take
-                clock = clock + take * pair_time
+    soft = [(0.25, prepare)] + [(0.46, None)] * pairs + [(0.4, turn)]
+    soft += [(1.7 / n, functools.partial(inner_tail, k)) for k in range(n)]
+    state = [0, 0.0, 0]
+
+    def fill(limit):
+        count = 0
+        while soft and state[1] + soft[0][0] <= limit:
+            cost, work = soft.pop(0)
+            state[1] += cost
+            if work is None:
+                count += 1
+                continue
+            if count:
+                lax.fori_loop(state[0], state[0] + count, body, 0)
+                state[0], count = state[0] + count, 0
+            work()
+        if count:
+            lax.fori_loop(state[0], state[0] + count, body, 0)
+            state[0] += count
+
+    whole = 1e9
+    begun = False
+    for time, index, cost, work in events:
+        if begun:
+            fill(whole if work.func in (finish_c, backward_tail) else time + 0.4)
+        if work.func is finish_b:
+            before_dt()
         work()
-        clock = max(clock, time)
-        if work.func is prepare:
+        state[1] = max(state[1], time) + cost
+        if work.func is pair_up and work.args == ("g", n - 1):
             begun = True
-            clock = time + 0.3
 
     for q, (plane, first, size, order) in enumerate(plan):
         unit = size
@@ -670,8 +766,6 @@
             gbc_ref[first : first + size, plane * TILE : (plane + 1) * TILE] = result
         else:
             last_ref[...] = result
-    for store in stores:
-        store.wait()
     for k in range(2):
         tot_copy(k).wait_send()
     for kind in kinds:
@@ -691,19 +785,28 @@
 
 
 def finish_kernel(heads, group, lanes, gvalues_in, glayer_in, gbc_in, last_in,
-                  gvalues_ref, glayer_ref, gbc_ref, gdt_ref, gbias_ref, grate_ref, gskip_ref):
-    gvalues_ref[...] = gvalues_in[...]
-    glayer_ref[...] = glayer_in[...]
-    gbc_ref[...] = gbc_in[...]
+                  gvalues_ref, glayer_ref, gbc_ref, gdt_ref, gbias_ref, grate_ref, gskip_ref, sems):
+    copies = [
+        pltpu.make_async_copy(source, target, sems.at[i])
+        for i, (source, target) in enumerate((
+            (gvalues_in, gvalues_ref), (glayer_in, glayer_ref), (gbc_in, gbc_ref),
+        ))
+    ]
+    for copy in copies:
+        copy.start()
     last = last_in[...]
-    share = gdt_ref.shape[0]
+    share = gdt_ref.shape[1]
+    pieces = []
     for j in range(lanes):
         count = min(share - j * group, group)
         if count > 0:
-            gdt_ref[j * group : j * group + count] = last[:count, j * heads : (j + 1) * heads]
+            pieces.append(last[:count, j * heads : (j + 1) * heads])
+    gdt_ref[...] = jnp.concatenate(pieces, axis=0).T
     gbias_ref[...] = last[group : group + 1, :heads]
     grate_ref[...] = last[group + 1 : group + 2, :heads]
     gskip_ref[...] = last[group + 2 : group + 3, :heads]
+    for copy in copies:
+        copy.wait()
 
 
 def local(layer_in, ssm_in, weight_bc, weight_dt, bias_dt, log_rate, skip_gain, grad_out):
@@ -718,13 +821,13 @@
     gvalues, glayer, gbc, last = pl.pallas_call(
         functools.partial(mega_kernel, devices, list(scratch)),
         out_shape=[
-            shape((tokens, width), BF16),
-            shape((tokens, depth), BF16),
-            shape((share, 2 * state_dim), F32),
-            shape((group + 8, TILE), F32),
+            pltpu.VMEM((tokens, width), BF16),
+            pltpu.VMEM((tokens, depth), BF16),
+            pltpu.VMEM((share, 2 * state_dim), F32),
+            pltpu.VMEM((group + 8, TILE), F32),
         ],
-        in_specs=[ANY] * 4 + [VMEM] * 3 + [ANY],
-        out_specs=[ANY, ANY, VMEM, VMEM],
+        in_specs=[ANY] * 8,
+        out_specs=[VMEM, VMEM, VMEM, VMEM],
         scratch_shapes=list(scratch.values()),
         compiler_params=pltpu.CompilerParams(
             collective_id=0, has_side_effects=True, vmem_limit_bytes=VMEM_LIMIT
@@ -738,17 +841,18 @@
             shape((tokens, width), BF16),
             shape((tokens, depth), BF16),
             shape((share, 2 * state_dim), F32),
-            shape((share, heads), F32),
+            shape((heads, share), F32),
             shape((1, heads), F32),
             shape((1, heads), F32),
             shape((1, heads), F32),
         ],
         in_specs=[VMEM] * 4,
-        out_specs=[VMEM] * 7,
-        compiler_params=pltpu.CompilerParams(vmem_limit_bytes=VMEM_LIMIT),
+        out_specs=[ANY] * 3 + [VMEM] * 4,
+        scratch_shapes=[pltpu.SemaphoreType.DMA((3,))],
+        compiler_params=pltpu.CompilerParams(vmem_limit_bytes=8 * 1024 * 1024),
         name="finish",
     )(gvalues, glayer, gbc, last)
-    return tuple(outs[:4]) + tuple(out[0] for out in outs[4:])
+    return tuple(outs[:3]) + (outs[3].T,) + tuple(out[0] for out in outs[4:])
 
 
 def solution(mesh):

time: 93.1 us -> 68.3 us (0.73)
  Pallas kernels: 90.7 us -> 67.3 us
  local copies, waits for them, and re-layouts: 1.58 us -> 0 us
    pallas_call x1, Pallas kernels: 87.3 us -> 65.2 us  [local(): pl.pallas_call(functools.partial(mega_kernel, devices, list(scratch)), ou...]
    unnamed x1 -> x0, local copies, waits for them, and re-layouts: 1.58 us -> none
    pallas_call x1, Pallas kernels: 3.38 us -> 2.18 us  [local(): pl.pallas_call(functools.partial(finish_kernel, heads, group, lanes), out...]
where the time goes in v2:
time: 68.3 us; the launch traced here: 68.2 us
  Pallas kernels  67.3 us (99%)
  between operations  0.8 us (1%)
    pallas_call x1, Pallas kernels, local(): pl.pallas_call(functools.partial(mega_kernel, devices, list(scratch)), ou...  65.2 us
    pallas_call x1, Pallas kernels, local(): pl.pallas_call(functools.partial(finish_kernel, heads, group, lanes), out...  2.18 us

profile of v2, /device:TPU:0, one launch (start us, length us, event | category | flops | bytes accessed | tf_op | source)
XLA Modules:
  0.0 68.2 jit_solution(3473452872149706690)
XLA Ops:
  0.6 65.2 %mixer.1 = (bf16[256,2560]{1,0:T(8,128)(2,1)S(1)}, bf16[256,2560]{1,0:T(8,128)(2,1)S(1)}, f32[160,256]{1,0:T(8,128)S(1)}, f32[64,128]{1,0:T(8,128)S(1)}) custom-call(bf16[256,2560]{1,0:T(8,128)(2,1)} %layer_hbm.1, bf16[256,2560]{1,0:T(8,128)(2,1)} %values_hbm.1, bf16[2560,256]{1,0:T(8,128)(2,1)} %wbc_hbm.1, bf16[40,2560]{1,0:T(8,128)(2,1)} %bitcast.8, ...), custom_call_target="tpu_custom_call" | custom-call | tf_op jit(solution)/shard_map/mixer/pallas_call | solution.py:821
  65.8 2.2 %finish.1 = (bf16[256,2560]{1,0:T(8,128)(2,1)}, bf16[256,2560]{1,0:T(8,128)(2,1)}, f32[160,256]{1,0:T(8,128)}, f32[40,160]{1,0:T(8,128)}, f32[1,40]{1,0:T(1,128)}, /*index=5*/f32[1,40]{1,0:T(1,128)}, f32[1,40]{1,0:T(1,128)}) custom-call(bf16[256,2560]{1,0:T(8,128)(2,1)S(1)} %get-tuple-element.18.gvalues_in, ...), custom_call_target="tpu_custom_call" | custom-call | tf_op jit(solution)/shard_map/finish/pallas_call | solution.py:838

commit v3 on v2

--- a/solution.py
+++ b/solution.py
@@ -11,7 +11,9 @@
 TILE = 128
 CHUNKS = 10
 BLOCK = 2
-REDUCE_C, REDUCE_B, REDUCE_DT = "zzyy", "yyyy", "z"
+TAILS = 4
+LOADS = 4
+REDUCE_C, REDUCE_B, REDUCE_DT = "zzyy", "yyyz", "z"
 VMEM_LIMIT = 52 * 1024 * 1024
 VMEM = pl.BlockSpec(memory_space=pltpu.VMEM)
 ANY = pl.BlockSpec(memory_space=pl.ANY)
@@ -211,7 +213,8 @@
         for i in range(levels):
             add(f"rget{q}_{i}", ((devices >> (i + 1)) * size, TILE))
     add_sem = lambda name, shape: names.__setitem__(name, pltpu.SemaphoreType.DMA(shape))
-    add_sem("load", (8,))
+    add_sem("load", (6,))
+    add_sem("early", (2, LOADS))
     add_sem("comm", (2, 5, 2, CHUNKS))
     add_sem("tot_sems", (2, 2))
     add_sem("rsem", (2, levels, len(plan)))
@@ -244,15 +247,30 @@
     down_row = lax.rem(me + devices - 4, devices)
     mesh_id = pl.DeviceIdType.MESH
 
+    pieces = [slice(i * depth // LOADS, (i + 1) * depth // LOADS) for i in range(LOADS)]
+    early = [
+        [
+            pltpu.make_async_copy(source, target, r.early.at[j, i])
+            for j, (source, target) in enumerate((
+                (layer_hbm.at[:, piece], r.layer.at[:, piece]),
+                (wbc_hbm.at[piece], r.wbc.at[piece]),
+            ))
+        ]
+        for i, piece in enumerate(pieces)
+    ]
     loads = [
         pltpu.make_async_copy(source, target, r.load.at[i])
         for i, (source, target) in enumerate((
-            (layer_hbm, r.layer), (wbc_hbm, r.wbc), (wdt_hbm, r.wdt),
+            (wdt_hbm, r.wdt), (bias_hbm, r.bias), (rate_hbm, r.rate), (gain_hbm, r.gain),
             (values_hbm, r.values), (grad_hbm, r.grad),
-            (bias_hbm, r.bias), (rate_hbm, r.rate), (gain_hbm, r.gain),
         ))
     ]
-    for i in (0, 1, 2, 5, 6, 7, 3, 4):
+    for i in range(4):
+        loads[i].start()
+    for group in early:
+        for load in group:
+            load.start()
+    for i in (4, 5):
         loads[i].start()
 
     barrier = pltpu.get_barrier_semaphore()
@@ -269,16 +287,22 @@
 
     r.hot[...] = one_hot(TILE, head_size, width)
     r.hot3[...] = one_hot_stacked(heads, head_size, width)
-    loads[0].wait()
-    loads[1].wait()
-    layer = r.layer[...]
-    proj = mm(layer, r.wbc[...]).astype(BF16)
+    for i in range(4):
+        loads[i].wait()
+    proj, raw = None, None
+    for piece, group in zip(pieces, early):
+        for load in group:
+            load.wait()
+        layer = r.layer[:, piece]
+        add_raw = mm_nt(layer, r.wdt[:, piece])
+        add_proj = mm(layer, r.wbc[piece])
+        proj = add_proj if proj is None else proj + add_proj
+        raw = add_raw if raw is None else raw + add_raw
+    raw = raw + r.bias[...]
+    r.raw[...] = raw
+    proj = proj.astype(BF16)
     r.proj[...] = proj
     r.proj_t[...] = proj.T
-    for i in (2, 5, 6, 7):
-        loads[i].wait()
-    raw = mm_nt(layer, r.wdt[...]) + r.bias[...]
-    r.raw[...] = raw
     step = jnp.maximum(raw, 0.0) + jnp.log1p(jnp.exp(-jnp.abs(raw)))
     r.step[...] = step
     decay = -jnp.exp(r.rate[...]) * step
@@ -357,7 +381,7 @@
 
     def make_states(kind, block):
         if block == 0:
-            loads[3 if kind == "s" else 4].wait()
+            loads[4 if kind == "s" else 5].wait()
         cols = slice(block * BLOCK * span, (block + 1) * BLOCK * span)
         hot = r.hot3[:, cols]
         if kind == "s":
@@ -614,10 +638,11 @@
             sums[start + group : start + unit] = small
         reduce_copy(q, 0).start()
 
-    def layer_tail():
-        glayer_ref[...] = (
-            mm_nt(r.gproj[:, : 2 * state_dim], r.wbc[...])
-            + mm(r.gproj[:, 2 * state_dim :], r.wdt[...])
+    def layer_tail(k):
+        cols = slice(k * depth // TAILS, (k + 1) * depth // TAILS)
+        glayer_ref[:, cols] = (
+            mm_nt(r.gproj[:, : 2 * state_dim], r.wbc[cols])
+            + mm(r.gproj[:, 2 * state_dim :], r.wdt[:, cols])
         ).astype(BF16)
 
     def prepare():
@@ -643,120 +668,143 @@
                    r.gu, r.rows, r.gscores, head_size)
         return 0
 
-    events = []
-
-    def event(time, cost, work, *args):
-        events.append((time, len(events), cost, functools.partial(work, *args)))
-
     n = CHUNKS
-    wire, flight, near, hop = 7.05 / n, 3.0, 1.05, 2.9 + 7.2 / n
-    start, blocks = 3.9, n // BLOCK
-    make_s, make_g = 2.25 / blocks, 1.95 / blocks
-    first = start + make_s + near
-    event(start + 2 * make_s - 0.01, 0.27, tot_done, 0)
-    event(first + 2.2, 0.25, tot_done, 1)
+    wire, flight, near, hop_wire, hop = 7.05 / n, 3.0, 1.1, 7.2 / (2 * n), 2.9 + 3.6 / n
+    blocks = n // BLOCK
+    pool, link = [], {"y": 0.0, "s": 0.0, "g": 0.0, "z": 0.0, "m": 0.0}
+    clock, serial = [3.2], [0]
+    left = {"s": n, "g": n}
+
+    def add(ready, rank, cost, work, args=(), after=None):
+        serial[0] += 1
+        pool.append((ready, rank, serial[0], cost, work, args, after))
+
+    def through(name, now, time):
+        link[name] = max(link[name], now) + time
+        return link[name]
+
+    def after_make(kind, block):
+        def after(now):
+            for k in range(block * BLOCK, (block + 1) * BLOCK):
+                add(now + near, 0, 0.02, pair_up, (kind, k), after_pair(kind, k))
+        return after
+
+    def after_pair(kind, k):
+        def after(now):
+            add(through("y", now, wire) + flight, 0, 0.02, row_up, (kind, k),
+                lambda now: add(now, 0, 0.01, chain_slot, (kind, k, 0), after_chain(kind, k, 0)))
+        return after
+
+    def after_chain(kind, k, place):
+        def after(now):
+            if place + 1 < zrows:
+                add(through(kind, now, hop_wire) + hop, 0, 0.01, chain_slot,
+                    (kind, k, place + 1), after_chain(kind, k, place + 1))
+            else:
+                add(now, 0, 0.02, row_down, (kind, k), after_down(kind, k))
+        return after
+
+    def after_down(kind, k):
+        def after(now):
+            add(through("y", now, wire) + flight, 0, 0.02, chip_down, (kind, k),
+                lambda now: add(now + near, 1, 4.1 / n if kind == "s" else 5.0 / n,
+                                forward_tail if kind == "s" else backward_tail, (k,),
+                                after_tail(kind)))
+        return after
+
+    def after_tail(kind):
+        def after(now):
+            left[kind] -= 1
+            if left[kind] == 0:
+                add(now, 1, 0.22, finish_c if kind == "s" else finish_b, (), after_finish(kind))
+        return after
+
+    def after_dt(now):
+        add(now, 1, 0.9, send_dt, (), after_send(len(plan) - 1))
+        for k in range(TAILS):
+            soft.append((1.5 / TAILS, functools.partial(layer_tail, k)))
+
+    def after_finish(kind):
+        def after(now):
+            for q, (plane, first, size, order) in enumerate(plan):
+                if plane == (1 if kind == "s" else 0):
+                    add(now, 1, size * 0.007, send_piece, (q,), after_send(q))
+            if kind == "g":
+                add(now + 0.01, 1, 0.31, finish_dt, (), after_dt)
+        return after
+
+    def after_send(q):
+        arrive = near + (0.5 if plan[q][0] == 2 else 0.0)
+        return lambda now: add(now + arrive, 0, 0.03, reduce_step, (q, 0), after_reduce(q, 0))
+
+    def after_reduce(q, i):
+        def after(now):
+            if i + 1 == levels:
+                return
+            level = plan[q][3][i + 1]
+            pace = plan[q][2] * 0.045 / (1 << i)
+            if level == 1:
+                arrive = through("y", now, pace) + 2.8
+            elif level == 2:
+                arrive = through("z", now, pace) + 2.8
+            else:
+                through("z", now, pace)
+                arrive = through("m", now, 2 * pace) + 3.5
+            if i + 2 == levels:
+                arrive += 1000.0
+            add(arrive, 0, 0.02, reduce_step, (q, i + 1), after_reduce(q, i + 1))
+        return after
+
     for block in range(blocks):
-        event(start + make_s * block, make_s, make_states, "s", block)
-        event(start + make_s * blocks + make_g * block, make_g, make_states, "g", block)
-    for k in range(n):
-        block = k // BLOCK
-        event(start + make_s * (block + 1) + near, 0.02, pair_up, "s", k)
-        event(start + make_s * blocks + make_g * (block + 1) + near + 0.3, 0.02, pair_up, "g", k)
-        for i, kind in enumerate(kinds):
-            arrive = first + wire * (i * n + k + 1) + flight
-            event(arrive, 0.02, row_up, kind, k)
-            for place in range(zrows):
-                event(arrive + hop * min(place, 3) + 0.01, 0.02, chain_slot, kind, k, place)
-            down = max(first + wire * (2 + i) * n, first + wire * (i * n + 1) + flight + 3 * hop)
-            down = down + wire * k
-            event(max(arrive + 3 * hop, down - 1.0) + 0.02, 0.02, row_down, kind, k)
-            event(down + wire + flight, 0.02, chip_down, kind, k)
-            arrive = down + wire + flight + near
-            if kind == "s":
-                event(arrive + 0.4, 3.4 / n, forward_tail, k)
-            else:
-                event(arrive + 0.2, 5.0 / n, backward_tail, k)
-            if k == n - 1 and kind == "s":
-                c_time = arrive + 0.5
-                event(c_time, 0.2, finish_c)
-            elif k == n - 1:
-                b_time = arrive + 0.3
-                event(b_time, 0.2, finish_b)
-                event(b_time + 1.5, 0.4, finish_dt)
-                event(b_time + 2.0, 0.8, send_dt)
-                event(b_time + 5.0, 1.4, layer_tail)
-    free = {"z": 0.0, "m": 0.0, "y": first + 4 * n * wire}
-    clocks = []
-    for q, (plane, offset_rows, size, order) in enumerate(plan):
-        piece = q % len(pieces_of(share))
-        if plane == 1:
-            made = c_time + 0.2 + 0.5 * piece
-        elif plane == 0:
-            made = b_time + 0.2 + 0.3 * piece
-        else:
-            made = b_time + 2.5
-        if plane < 2:
-            event(made, 0.3, send_piece, q)
-        ready = made + 0.3 + 1.1
-        if plane == 1 and order[1] == 1:
-            ready = max(ready, down + 0.1)
-        clocks.append([ready, size * 0.045])
-        event(clocks[q][0], 0.04, reduce_step, q, 0)
-    pending = [(clocks[q][0], q, 1) for q in range(len(plan))]
-    while pending:
-        pending.sort()
-        ready, q, i = pending.pop(0)
-        level = plan[q][3][i]
-        pace = clocks[q][1]
-        clocks[q][1] = pace / 2
-        begin = max(ready, free["y" if level == 1 else "z"])
-        if level == 1:
-            free["y"] = begin + pace
-            done_at = begin + pace + 2.8
-        elif level == 2:
-            free["z"] = begin + pace
-            done_at = begin + pace + 2.8
-        else:
-            free["z"] = begin + pace
-            free["m"] = max(begin, free["m"]) + 2 * pace
-            done_at = free["m"] + 3.5
-        event(done_at, 0.03, reduce_step, q, i)
-        if i + 1 < levels:
-            pending.append((done_at, q, i + 1))
-    events.sort(key=lambda item: item[:2])
+        add(0.0, 1, 2.25 / blocks, make_states, ("s", block), after_make("s", block))
+    for block in range(blocks):
+        add(0.1, 1, 1.9 / blocks, make_states, ("g", block), after_make("g", block))
+    add(4.0, 0, 0.25, tot_done, (0,))
+    add(7.0, 0, 0.25, tot_done, (1,))
 
     pairs = width // TILE
     soft = [(0.25, prepare)] + [(0.46, None)] * pairs + [(0.4, turn)]
-    soft += [(1.7 / n, functools.partial(inner_tail, k)) for k in range(n)]
-    state = [0, 0.0, 0]
-
-    def fill(limit):
-        count = 0
-        while soft and state[1] + soft[0][0] <= limit:
-            cost, work = soft.pop(0)
-            state[1] += cost
-            if work is None:
-                count += 1
-                continue
-            if count:
-                lax.fori_loop(state[0], state[0] + count, body, 0)
-                state[0], count = state[0] + count, 0
+    soft += [(1.7 / n, functools.partial(inner_tail, k)) for k in range(n)] + [(0.4, before_dt)]
+    pending = [0, 0]
+
+    def flush_pairs():
+        if pending[1]:
+            lax.fori_loop(pending[0], pending[0] + pending[1], body, 0)
+            pending[0], pending[1] = pending[0] + pending[1], 0
+
+    def soften():
+        cost, work = soft.pop(0)
+        clock[0] += cost
+        if work is None:
+            pending[1] += 1
+        else:
+            flush_pairs()
             work()
-        if count:
-            lax.fori_loop(state[0], state[0] + count, body, 0)
-            state[0] += count
-
-    whole = 1e9
-    begun = False
-    for time, index, cost, work in events:
-        if begun:
-            fill(whole if work.func in (finish_c, backward_tail) else time + 0.4)
-        if work.func is finish_b:
-            before_dt()
-        work()
-        state[1] = max(state[1], time) + cost
-        if work.func is pair_up and work.args == ("g", n - 1):
-            begun = True
+
+    while pool:
+        ready = [item for item in pool if item[0] <= clock[0] + 1e-6]
+        if not ready:
+            following = min(item[0] for item in pool)
+            usable = soft and (soft[0][1] is not before_dt or left["s"] == 0)
+            if usable and clock[0] + soft[0][0] <= following + 0.25:
+                soften()
+            else:
+                clock[0] = following
+            continue
+        item = min(ready, key=lambda entry: (entry[1], entry[0], entry[2]))
+        pool.remove(item)
+        cost, work, args, after = item[3:]
+        if work in (finish_c, backward_tail):
+            while soft and soft[0][1] is not before_dt:
+                soften()
+        if work is finish_dt or item[0] > 1000.0:
+            while soft:
+                soften()
+        flush_pairs()
+        work(*args)
+        clock[0] += cost
+        if after:
+            after(clock[0])
 
     for q, (plane, first, size, order) in enumerate(plan):
         unit = size

time: 68.3 us -> 66.3 us (0.971)
  Pallas kernels: 67.3 us -> 65.4 us
    pallas_call x1, Pallas kernels: 65.2 us -> 63.2 us  [local(): pl.pallas_call(functools.partial(mega_kernel, devices, list(scratch)), ou...]
where the time goes in v3:
time: 66.3 us; the launch traced here: 66.2 us
  Pallas kernels  65.4 us (99%)
  between operations  0.8 us (1%)
    pallas_call x1, Pallas kernels, local(): pl.pallas_call(functools.partial(mega_kernel, devices, list(scratch)), ou...  63.2 us
    pallas_call x1, Pallas kernels, local(): pl.pallas_call(functools.partial(finish_kernel, heads, group, lanes), out...  2.18 us

profile of v3, /device:TPU:0, one launch (start us, length us, event | category | flops | bytes accessed | tf_op | source)
XLA Modules:
  0.0 66.2 jit_solution(6367742086021117366)
XLA Ops:
  0.6 63.2 %mixer.1 = (bf16[256,2560]{1,0:T(8,128)(2,1)S(1)}, bf16[256,2560]{1,0:T(8,128)(2,1)S(1)}, f32[160,256]{1,0:T(8,128)S(1)}, f32[64,128]{1,0:T(8,128)S(1)}) custom-call(bf16[256,2560]{1,0:T(8,128)(2,1)} %layer_hbm.1, bf16[256,2560]{1,0:T(8,128)(2,1)} %values_hbm.1, bf16[2560,256]{1,0:T(8,128)(2,1)} %wbc_hbm.1, bf16[40,2560]{1,0:T(8,128)(2,1)} %bitcast.8, ...), custom_call_target="tpu_custom_call" | custom-call | tf_op jit(solution)/shard_map/mixer/pallas_call | solution.py:869
  63.8 2.2 %finish.1 = (bf16[256,2560]{1,0:T(8,128)(2,1)}, bf16[256,2560]{1,0:T(8,128)(2,1)}, f32[160,256]{1,0:T(8,128)}, f32[40,160]{1,0:T(8,128)}, f32[1,40]{1,0:T(1,128)}, /*index=5*/f32[1,40]{1,0:T(1,128)}, f32[1,40]{1,0:T(1,128)}) custom-call(bf16[256,2560]{1,0:T(8,128)(2,1)S(1)} %get-tuple-element.18.gvalues_in, ...), custom_call_target="tpu_custom_call" | custom-call | tf_op jit(solution)/shard_map/finish/pallas_call | solution.py:886

commit v4 on v3

--- a/solution.py
+++ b/solution.py
@@ -669,7 +669,7 @@
         return 0
 
     n = CHUNKS
-    wire, flight, near, hop_wire, hop = 7.05 / n, 3.0, 1.1, 7.2 / (2 * n), 2.9 + 3.6 / n
+    wire, flight, near, hop_wire, hop = 7.05 / n, 2.7, 1.0, 7.2 / (2 * n), 2.7 + 3.6 / n
     blocks = n // BLOCK
     pool, link = [], {"y": 0.0, "s": 0.0, "g": 0.0, "z": 0.0, "m": 0.0}
     clock, serial = [3.2], [0]

time: 66.3 us -> 65.6 us (0.989)
  Pallas kernels: 65.4 us -> 64.7 us
    pallas_call x1, Pallas kernels: 63.2 us -> 62.5 us  [local(): pl.pallas_call(functools.partial(mega_kernel, devices, list(scratch)), ou...]
where the time goes in v4:
time: 65.6 us; the launch traced here: 65.5 us
  Pallas kernels  64.7 us (99%)
  between operations  0.8 us (1%)
    pallas_call x1, Pallas kernels, local(): pl.pallas_call(functools.partial(mega_kernel, devices, list(scratch)), ou...  62.5 us
    pallas_call x1, Pallas kernels, local(): pl.pallas_call(functools.partial(finish_kernel, heads, group, lanes), out...  2.18 us

profile of v4, /device:TPU:0, one launch (start us, length us, event | category | flops | bytes accessed | tf_op | source)
XLA Modules:
  0.0 65.5 jit_solution(8643374760634965017)
XLA Ops:
  0.6 62.5 %mixer.1 = (bf16[256,2560]{1,0:T(8,128)(2,1)S(1)}, bf16[256,2560]{1,0:T(8,128)(2,1)S(1)}, f32[160,256]{1,0:T(8,128)S(1)}, f32[64,128]{1,0:T(8,128)S(1)}) custom-call(bf16[256,2560]{1,0:T(8,128)(2,1)} %layer_hbm.1, bf16[256,2560]{1,0:T(8,128)(2,1)} %values_hbm.1, bf16[2560,256]{1,0:T(8,128)(2,1)} %wbc_hbm.1, bf16[40,2560]{1,0:T(8,128)(2,1)} %bitcast.8, ...), custom_call_target="tpu_custom_call" | custom-call | tf_op jit(solution)/shard_map/mixer/pallas_call | solution.py:869
  63.1 2.2 %finish.1 = (bf16[256,2560]{1,0:T(8,128)(2,1)}, bf16[256,2560]{1,0:T(8,128)(2,1)}, f32[160,256]{1,0:T(8,128)}, f32[40,160]{1,0:T(8,128)}, f32[1,40]{1,0:T(1,128)}, /*index=5*/f32[1,40]{1,0:T(1,128)}, f32[1,40]{1,0:T(1,128)}) custom-call(bf16[256,2560]{1,0:T(8,128)(2,1)S(1)} %get-tuple-element.18.gvalues_in, ...), custom_call_target="tpu_custom_call" | custom-call | tf_op jit(solution)/shard_map/finish/pallas_call | solution.py:886
